TPU v7x, 32 devices: a whole 2x2x4 slice. The times are simulated.
32 devices in a mesh: gx: 4 (over x, core), gy: 4 (over z), gz: 2 (over y).
Axes of the slice: x: 2, y: 2, z: 4, core: 2. Of those that a mesh axis runs over, the one named last changes fastest.
Arguments:
- occupied: float32 [16, 16, 16, 256], P(None, 'gx', 'gy', 'gz'), may hold values from -6 to 6
- virtual: float32 [16, 16, 16, 256], P(None, 'gx', 'gy', 'gz'), may hold values from -6 to 6
- kernel_fields: float32 [4, 16, 16, 256], P(None, 'gx', 'gy', 'gz'), may hold values from -1.5 to 1.5
- density_grad: float32 [3, 16, 16, 256], P(None, 'gx', 'gy', 'gz'), may hold values from -6 to 6
Outputs:
- potential: float32 [256, 16, 16, 256], P(None, 'gx', 'gy', 'gz')
- casida: float32 [256, 256], P(('gx', 'gy', 'gz'))
All inputs are finite; a program needn't handle non-finite values.
Results may differ from a plain program's by a relative error of at most 0.00013.
Values sent between devices are 32-bit elements; how exact they have to be, the bound alone decides.
A program may use at most 64 MiB of HBM per device.

v0:
```python
import functools

import jax
import jax.numpy as jnp
from jax import lax
from jax.experimental import pallas as pl
from jax.experimental.pallas import tpu as pltpu
from jax.sharding import PartitionSpec as P

MESH = pl.DeviceIdType.MESH
F32 = jnp.float32
BF16 = jnp.bfloat16


def spread(v, lane):
    lanes = v.shape[1]
    v = jnp.where((lane < 4) | (lane >= lanes - 4), v, 0.0)
    step = 8
    while step < lanes:
        turns = [pltpu.roll(v, k * step, 1) for k in range(1, 4) if k * step < lanes]
        for t in turns:
            v = v + t
        step *= 4
    return v


def slot_owner(shape):
    lane = lax.broadcasted_iota(jnp.int32, shape, 1)
    row = lax.broadcasted_iota(jnp.int32, shape, 0)
    return lax.rem(((lane + 4) // 8) + row, shape[1] // 8) == 0


def prep_kernel(cells, occ, vir, ker, grd, orb, fld, zed, zfl):
    lanes = occ.shape[1]
    nocc, nvir = occ.shape[0] // cells, vir.shape[0] // cells

    def cell(c, carry):
        for k, (ref, count, at) in enumerate(((occ, nocc, 0), (vir, nvir, nocc))):
            rows = ref[pl.ds(c, count, stride=cells), :]
            orb[c, at:at + count] = rows
            lane = lax.broadcasted_iota(jnp.int32, rows.shape, 1)
            packed = jnp.where(slot_owner(rows.shape), spread(rows, lane), 0.0)
            zed[c, k:k + 1] = jnp.sum(packed, axis=0, keepdims=True)
        g = [grd[pl.ds(k * cells + c, 1), :] for k in range(3)]
        f = [ker[pl.ds(k * cells + c, 1), :] for k in range(4)]
        rows = g + [f[1] * (1.0 / 12.0), f[2] * (1.0 / 144.0), f[3] * (1.0 / 144.0), f[0], f[0]]
        eight = jnp.concatenate(rows, axis=0)
        fld[c] = eight
        zfl[c] = spread(eight, lax.broadcasted_iota(jnp.int32, eight.shape, 1))
        return carry

    lax.fori_loop(0, cells, cell, 0, unroll=4)


def halo_kernel(orb, fld, zed, zfl, wide, wfld, wz, wg, send, recv, own):
    nx, ny, nz = (lax.axis_size(a) for a in ("gx", "gy", "gz"))
    x, y, z = (lax.axis_index(a) for a in ("gx", "gy", "gz"))
    bx, by = orb.shape[0], orb.shape[1]
    up = lambda v, n: lax.rem(v + 1, n)
    dn = lambda v, n: lax.rem(v + n - 1, n)
    xs = (dn(x, nx), up(x, nx))
    ys = (dn(y, ny), up(y, ny))
    zs = (dn(z, nz), up(z, nz))

    def dev(gx=None, gy=None, gz=None):
        return {
            "gx": x if gx is None else gx,
            "gy": y if gy is None else gy,
            "gz": z if gz is None else gz,
        }

    barrier = pltpu.get_barrier_semaphore()
    others = [dev(gx=v) for v in xs] + [dev(gy=v) for v in ys] + [dev(gz=v) for v in zs]
    for d in others:
        pl.semaphore_signal(barrier, inc=1, device_id=d, device_id_type=MESH)
    pl.semaphore_wait(barrier, len(others))

    copies = []

    def put(src, dst, device):
        k = len(copies)
        c = pltpu.make_async_remote_copy(
            src_ref=src,
            dst_ref=dst,
            send_sem=send.at[k],
            recv_sem=recv.at[k],
            device_id=device,
            device_id_type=MESH,
        )
        c.start()
        copies.append(c)
        return c

    def edge(b, side, width):
        return pl.ds(b - width, width) if side == 0 else pl.ds(0, width)

    def rim(b, side, width, margin):
        return pl.ds(margin - width, width) if side == 0 else pl.ds(b + margin, width)

    in_x, in_y = pl.ds(4, bx), pl.ds(4, by)
    mid_x, mid_y = pl.ds(2, bx), pl.ds(2, by)
    near = [
        put(
            orb.at[:, edge(by, side, 2)],
            wide.at[in_x, rim(by, side, 2, 4)],
            dev(gy=ys[1 - side]),
        )
        for side in range(2)
    ]
    zc = []
    for side in range(2):
        zc.append(put(zed, wz.at[side, mid_x, mid_y], dev(gz=zs[1 - side])))
        put(zfl, wg.at[side], dev(gz=zs[1 - side]))
    for side in range(2):
        put(
            orb,
            wide.at[pl.ds(0, bx) if side == 0 else pl.ds(bx + 4, bx), in_y],
            dev(gx=xs[1 - side]),
        )
        far_src = pl.ds(by - 4, 2) if side == 0 else pl.ds(2, 2)
        far_dst = pl.ds(0, 2) if side == 0 else pl.ds(by + 6, 2)
        put(orb.at[:, far_src], wide.at[in_x, far_dst], dev(gy=ys[1 - side]))
        put(
            fld.at[edge(bx, side, 2)],
            wfld.at[rim(bx, side, 2, 2), mid_y],
            dev(gx=xs[1 - side]),
        )
        put(
            fld.at[:, edge(by, side, 2)],
            wfld.at[mid_x, rim(by, side, 2, 2)],
            dev(gy=ys[1 - side]),
        )
    mine = [
        pltpu.make_async_copy(orb, wide.at[in_x, in_y], own.at[0]),
        pltpu.make_async_copy(fld, wfld.at[mid_x, mid_y], own.at[1]),
    ]
    for c in mine:
        c.start()
    for c in zc:
        c.wait_recv()
    last = []
    for side in range(2):
        own_x = pl.ds(bx, 2) if side == 0 else pl.ds(2, 2)
        own_y = pl.ds(by, 2) if side == 0 else pl.ds(2, 2)
        for k in range(2):
            last.append(
                put(
                    wz.at[k, own_x, mid_y],
                    wz.at[k, rim(bx, side, 2, 2), mid_y],
                    dev(gx=xs[1 - side]),
                )
            )
            last.append(
                put(
                    wz.at[k, mid_x, own_y],
                    wz.at[k, mid_x, rim(by, side, 2, 2)],
                    dev(gy=ys[1 - side]),
                )
            )
    for sy in range(2):
        near[sy].wait_recv()
        for sx in range(2):
            own_x = pl.ds(bx + 2, 2) if sx == 0 else pl.ds(4, 2)
            rim_y = rim(by, sy, 2, 4)
            put(
                wide.at[own_x, rim_y],
                wide.at[rim(bx, sx, 2, 4), rim_y],
                dev(gx=xs[1 - sx]),
            )
    early = near + zc
    for c in early:
        c.wait_send()
    for c in copies:
        if not any(c is e for e in early):
            c.wait()
    for c in mine:
        c.wait()


def main_kernel(
    norb, wide, wfld, wz, wg,
    pot, part,
    nS, oS, vS, vE, eF, C, A0, A1, f0, f1, f2, base, ph, plo, nh, nl,
):
    nocc, nvir = norb
    bx, by = wide.shape[0] - 8, wide.shape[1] - 8
    lanes = wide.shape[3]
    i = pl.program_id(0)
    shifts = (1, -1, 2, -2)

    center = [(x, y) for x in range(bx) for y in range(by)]
    xarm = [(x, y) for x in (-2, -1, bx, bx + 1) for y in range(by)]
    yarm = [(x, y) for x in range(bx) for y in (-2, -1, by, by + 1)]
    near = center + xarm + yarm
    far = [(x, y) for x in (-4, -3, bx + 2, bx + 3) for y in range(by)]
    far += [(x, y) for x in range(bx) for y in (-4, -3, by + 2, by + 3)]
    far += [(x, y) for x in (-2, -1, bx, bx + 1) for y in (-2, -1, by, by + 1)]
    lane = lax.broadcasted_iota(jnp.int32, (nvir, lanes), 1)

    def slope(f):
        return 8.0 * (f(1) - f(-1)) - (f(2) - f(-2))

    @pl.when(i == 0)
    def _():
        lane1 = lax.broadcasted_iota(jnp.int32, (1, lanes), 1)
        upper = (lane1 & 7) < 4
        owner = slot_owner((nocc, lanes))

        def wrapped(s):
            return lane < s if s > 0 else lane >= lanes + s

        def pair(x, y):
            rows = jnp.where(upper, wz[1, x, y], wz[0, x, y])
            alt = [
                pltpu.roll(
                    jnp.broadcast_to(rows[k:k + 1], (n, lanes)), 0, 1, stride=8, stride_axis=0
                )
                for k, n in enumerate((nocc, nvir))
            ]
            return rows, alt, wide[x + 2, y + 2, 0:nocc], wide[x + 2, y + 2, nocc:nocc + nvir]

        def prepare(x, y):
            rows, (o_alt, v_alt), o_own, v_own = pair(x, y)
            vE[0, x, y] = rows[0:1] * spread(v_alt, lane)
            for k, s in enumerate(shifts):
                m = wrapped(s)
                roll = (-s) % lanes
                scale = 8.0 if abs(s) == 1 else 1.0
                oS[k, x, y] = scale * pltpu.roll(jnp.where(m, o_alt, o_own), roll, 1)
                vS[k, x, y] = pltpu.roll(jnp.where(m, v_alt, v_own), roll, 1)

        def band(t, c):
            prepare(t // by, 2 + lax.rem(t, by))
            return c

        lax.fori_loop(0, (bx + 4) * by, band, 0, unroll=4)

        def sides(t, c):
            y = lax.rem(t, 4)
            prepare(2 + t // 4, jnp.where(y < 2, y, y + by))
            return c

        lax.fori_loop(0, bx * 4, sides, 0, unroll=4)

        def flux_at(me, f, s, n):
            g = [f[k:k + 1] for k in range(3)]
            total = (f[3:4] * g[me]) * n
            for k in range(3):
                c = f[4:5] * g[me] * g[k]
                total += (c + f[5:6] if k == me else c) * s[k]
            return total

        def edges(t, carry):
            x, y = t // by + 2, lax.rem(t, by) + 2
            rows, (o_alt, v_alt), o_own, v_own = pair(x, y)
            p = []
            for k, s in enumerate(shifts):
                m = wrapped(s)
                roll = (-s) % lanes
                oe = spread(pltpu.roll(jnp.where(m, o_own, o_alt), roll, 1), lane)
                ve = spread(pltpu.roll(jnp.where(m, v_own, v_alt), roll, 1), lane)
                oe = jnp.sum(jnp.where(owner, oe, 0.0), axis=0, keepdims=True)
                p.append(oe * ve)
            s2 = 8.0 * (p[0] - p[1]) - (p[2] - p[3])
            s0 = slope(lambda d: vE[0, x + d, y])
            s1 = slope(lambda d: vE[0, x, y + d])
            g = jnp.where(upper, wg[1, x - 2, y - 2], wg[0, x - 2, y - 2])
            eF[x - 2, y - 2] = flux_at(2, g, (s0, s1, s2), vE[0, x, y])
            f = wfld[x, y]
            for k in range(7):
                C[k, x - 2, y - 2] = jnp.broadcast_to(f[k:k + 1], (8, lanes))
            return carry

        lax.fori_loop(0, bx * by, edges, 0, unroll=4)

        def arm_coefs(arm, at, me, f):
            gm = f[me:me + 1]
            for k in range(3):
                c = f[4:5] * gm * f[k:k + 1]
                if k == me:
                    c = c + f[5:6]
                arm[k, at] = jnp.broadcast_to(c, (8, lanes))
            arm[3, at] = jnp.broadcast_to(f[3:4] * gm, (8, lanes))

        def arm_x(t, c):
            x = t // by
            arm_coefs(A0, t, 0, wfld[jnp.where(x < 2, x, x + bx), 2 + lax.rem(t, by)])
            return c

        lax.fori_loop(0, 4 * by, arm_x, 0, unroll=4)

        def arm_y(t, c):
            y = lax.rem(t, 4)
            arm_coefs(A1, t, 1, wfld[2 + t // 4, jnp.where(y < 2, y, y + by)])
            return c

        lax.fori_loop(0, 4 * bx, arm_y, 0, unroll=4)

    def rows2(c):
        return jnp.concatenate([c] * (nvir // 8), axis=0)

    off = 4
    for x, y in near + far:
        cell = wide.at[x + off, y + off]
        nS[x + off, y + off] = cell[pl.ds(i, 1)] * cell[nocc:nocc + nvir]

    def n_at(x, y):
        return nS[x + off, y + off]

    def slopes(x, y):
        s0 = slope(lambda t: n_at(x + t, y))
        s1 = slope(lambda t: n_at(x, y + t))
        p = [oS[k, x + 2, y + 2, pl.ds(i, 1)] * vS[k, x + 2, y + 2] for k in range(4)]
        return s0, s1, (p[0] - p[1]) - (p[2] - p[3])

    for arm, cells, out in ((A0, xarm, f0), (A1, yarm, f1)):
        for at, (x, y) in enumerate(cells):
            s0, s1, s2 = slopes(x, y)
            value = (
                rows2(arm[0, at]) * s0
                + rows2(arm[1, at]) * s1
                + rows2(arm[2, at]) * s2
                + rows2(arm[3, at]) * n_at(x, y)
            )
            if out is f0:
                f0[x + 2, y] = value
            else:
                f1[x, y + 2] = value

    back = 8 * i
    row0 = pl.multiple_of(i * nvir, nvir)
    for x, y in center:
        s0, s1, s2 = slopes(x, y)
        g0, g1, g2, k1, k2, k3, kk = (rows2(C[k, x, y]) for k in range(7))
        n = n_at(x, y)
        al = g0 * s0 + g1 * s1 + g2 * s2
        sc = k1 * n + k2 * al
        f0[x + 2, y] = sc * g0 + k3 * s0
        f1[x, y + 2] = sc * g1 + k3 * s1
        f = sc * g2 + k3 * s2
        e = pltpu.roll(eF[x, y], back, 1)
        up1 = pltpu.roll(jnp.where(lane < 1, e, f), lanes - 1, 1)
        up2 = pltpu.roll(jnp.where(lane < 2, e, f), lanes - 2, 1)
        dn1 = pltpu.roll(jnp.where(lane >= lanes - 1, e, f), 1, 1)
        dn2 = pltpu.roll(jnp.where(lane >= lanes - 2, e, f), 2, 1)
        base[x, y] = kk * n + k1 * al - (8.0 * (up1 - dn1) - (up2 - dn2))
        at = (x * by + y) * lanes
        hi = n.astype(BF16)
        nh[pl.ds(row0, nvir), at:at + lanes] = hi
        nl[pl.ds(row0, nvir), at:at + lanes] = (n - hi.astype(F32)).astype(BF16)

    for x, y in center:
        inner = (f0[x + 3, y] - f0[x + 1, y]) + (f1[x, y + 3] - f1[x, y + 1])
        outer = (f0[x + 4, y] - f0[x, y]) + (f1[x, y + 4] - f1[x, y])
        v = base[x, y] - (8.0 * inner - outer)
        cell = x * by + y
        pot[pl.ds(cell, nvir, stride=bx * by), :] = v
        at = cell * lanes
        hi = v.astype(BF16)
        ph[pl.ds(row0, nvir), at:at + lanes] = hi
        plo[pl.ds(row0, nvir), at:at + lanes] = (v - hi.astype(F32)).astype(BF16)

    @pl.when(i == nocc - 1)
    def _():
        def dot(a, b):
            return lax.dot_general(
                a[...], b[...], (((1,), (1,)), ((), ())), preferred_element_type=F32
            )

        part[...] = dot(nh, ph) + dot(nh, plo) + dot(nl, ph)


def scatter_kernel(scale, part, out, got, acc, got2, send, recv, send2, recv2):
    nx, ny, nz = (lax.axis_size(a) for a in ("gx", "gy", "gz"))
    x, y, z = (lax.axis_index(a) for a in ("gx", "gy", "gz"))
    n = nx * nz
    me = x * nz + z

    def plane(d):
        t = lax.rem(me + d, n)
        tx, tz = t // nz, lax.rem(t, nz)
        return tx, tz, {"gx": tx, "gy": y, "gz": tz}

    def column(d):
        t = lax.rem(y + d, ny)
        return t, {"gx": x, "gy": t, "gz": z}

    barrier = pltpu.get_barrier_semaphore()
    for d in range(1, n):
        pl.semaphore_signal(barrier, inc=1, device_id=plane(d)[2], device_id_type=MESH)
    for d in range(1, ny):
        pl.semaphore_signal(barrier, inc=1, device_id=column(d)[1], device_id_type=MESH)
    pl.semaphore_wait(barrier, n - 1 + ny - 1)

    first = []
    for d in range(1, n):
        tx, tz, target = plane(d)
        c = pltpu.make_async_remote_copy(
            src_ref=part.at[tx, :, tz],
            dst_ref=got.at[d],
            send_sem=send.at[d],
            recv_sem=recv.at[d],
            device_id=target,
            device_id_type=MESH,
        )
        c.start()
        first.append(c)
    total = part[x, :, z]
    for d, c in enumerate(first):
        c.wait_recv()
        total = total + got[d + 1]
    acc[...] = total
    second = []
    for d in range(1, ny):
        t, target = column(d)
        c = pltpu.make_async_remote_copy(
            src_ref=acc.at[t],
            dst_ref=got2.at[d],
            send_sem=send2.at[d],
            recv_sem=recv2.at[d],
            device_id=target,
            device_id_type=MESH,
        )
        c.start()
        second.append(c)
    for c in first:
        c.wait_send()
    total = acc[y]
    for d, c in enumerate(second):
        c.wait()
        total = total + got2[d + 1]
    out[...] = total * scale


def on_device(occupied, virtual, kernel_fields, density_grad):
    nocc, bx, by, lanes = occupied.shape
    nvir = virtual.shape[0]
    nx, ny, nz = (lax.axis_size(a) for a in ("gx", "gy", "gz"))
    devices = nx * ny * nz
    sds = lambda *s: jax.ShapeDtypeStruct(s, F32)
    norb = nocc + nvir
    vmem = pl.BlockSpec(memory_space=pltpu.VMEM)
    plane = bx * by
    flat = lambda a: a.reshape(-1, lanes)
    orb, fld, zed, zfl = pl.pallas_call(
        functools.partial(prep_kernel, plane),
        out_shape=(
            sds(plane, norb, lanes),
            sds(plane, 8, lanes),
            sds(plane, 2, lanes),
            sds(plane, 8, lanes),
        ),
        in_specs=[vmem] * 4,
        out_specs=[vmem] * 4,
        compiler_params=pltpu.CompilerParams(vmem_limit_bytes=8 * 1024 * 1024),
        name="prep",
    )(flat(occupied), flat(virtual), flat(kernel_fields), flat(density_grad))
    by_cell = lambda a: a.reshape((bx, by) + a.shape[1:])

    halos = pl.pallas_call(
        halo_kernel,
        out_shape=(
            sds(bx + 8, by + 8, norb, lanes),
            sds(bx + 4, by + 4, 8, lanes),
            sds(2, bx + 4, by + 4, 2, lanes),
            sds(2, bx, by, 8, lanes),
        ),
        in_specs=[pl.BlockSpec(memory_space=pl.ANY)] * 4,
        out_specs=[pl.BlockSpec(memory_space=pl.ANY)] * 4,
        scratch_shapes=[
            pltpu.SemaphoreType.DMA((26,)),
            pltpu.SemaphoreType.DMA((26,)),
            pltpu.SemaphoreType.DMA((2,)),
        ],
        compiler_params=pltpu.CompilerParams(
            collective_id=0, has_side_effects=True, vmem_limit_bytes=8 * 1024 * 1024
        ),
        name="halo",
    )(by_cell(orb), by_cell(fld), by_cell(zed), by_cell(zfl))

    cells = bx * by * lanes
    pairs = nocc * nvir
    wide = lambda *s: pltpu.VMEM(s + (nvir, lanes), F32)
    pot, part = pl.pallas_call(
        functools.partial(main_kernel, (nocc, nvir)),
        grid=(nocc,),
        out_shape=(sds(pairs * bx * by, lanes), sds(pairs, pairs)),
        in_specs=[vmem] * 4,
        out_specs=(
            pl.BlockSpec((nvir * bx * by, lanes), lambda i: (i, 0)),
            pl.BlockSpec((pairs, pairs), lambda i: (0, 0)),
        ),
        scratch_shapes=[
            wide(bx + 8, by + 8),
            pltpu.VMEM((4, bx + 4, by + 4, nocc, lanes), F32),
            wide(4, bx + 4, by + 4),
            wide(1, bx + 4, by + 4),
            wide(bx, by),
            pltpu.VMEM((7, bx, by, 8, lanes), F32),
            pltpu.VMEM((4, 4 * by, 8, lanes), F32),
            pltpu.VMEM((4, 4 * bx, 8, lanes), F32),
            wide(bx + 4, by),
            wide(bx, by + 4),
            wide(1),
            wide(bx, by),
        ]
        + [pltpu.VMEM((pairs, cells), BF16)] * 4,
        compiler_params=pltpu.CompilerParams(
            dimension_semantics=("arbitrary",), vmem_limit_bytes=28 * 1024 * 1024
        ),
        name="response",
    )(*halos)

    rows = pairs // devices
    casida = pl.pallas_call(
        functools.partial(scatter_kernel, 1.0 / (cells * devices)),
        out_shape=sds(rows, pairs),
        in_specs=[vmem],
        out_specs=vmem,
        scratch_shapes=[
            pltpu.VMEM((nx * nz, ny, rows, pairs), F32),
            pltpu.VMEM((ny, rows, pairs), F32),
            pltpu.VMEM((ny, rows, pairs), F32),
            pltpu.SemaphoreType.DMA((nx * nz,)),
            pltpu.SemaphoreType.DMA((nx * nz,)),
            pltpu.SemaphoreType.DMA((ny,)),
            pltpu.SemaphoreType.DMA((ny,)),
        ],
        compiler_params=pltpu.CompilerParams(collective_id=1, has_side_effects=True),
        name="scatter",
    )(part.reshape(nx, ny, nz, rows, pairs))
    return pot.reshape(pairs, bx, by, lanes), casida


def solution(mesh):
    spec = P(None, "gx", "gy", "gz")
    return jax.shard_map(
        on_device,
        mesh=mesh,
        in_specs=(spec,) * 4,
        out_specs=(spec, P(("gx", "gy", "gz"), None)),
        check_vma=False,
    )
```

profile of v0, /device:TPU:0, one launch (start us, length us, event | category | flops | bytes accessed | tf_op | source)
XLA Modules:
  0.0 66.4 jit_solution(2575997745040549596)
XLA Ops:
  0.6 0.0 copy-start.1
  0.6 0.9 %copy-done.1 = f32[16,4,4,128]{3,2,1,0:T(4,128)S(1)} copy-done((f32[16,4,4,128]{3,2,1,0:T(4,128)S(1)}, f32[16,4,4,128]{3,2,1,0:T(4,128)}, u32[]{:S(2)}) %copy-start.1) | copy-done | bytes 131096
  1.5 0.0 copy-start.2
  1.5 0.9 %copy-done.2 = f32[16,4,4,128]{3,2,1,0:T(4,128)S(1)} copy-done((f32[16,4,4,128]{3,2,1,0:T(4,128)S(1)}, f32[16,4,4,128]{3,2,1,0:T(4,128)}, u32[]{:S(2)}) %copy-start.2) | copy-done | bytes 131096
  2.4 0.0 copy-start.3
  2.4 0.8 %copy-done.3 = f32[4,4,4,128]{3,2,1,0:T(4,128)S(1)} copy-done((f32[4,4,4,128]{3,2,1,0:T(4,128)S(1)}, f32[4,4,4,128]{3,2,1,0:T(4,128)}, u32[]{:S(2)}) %copy-start.3) | copy-done | bytes 32792
  3.2 0.0 copy-start.4
  3.2 0.7 %copy-done.4 = f32[3,4,4,128]{3,2,1,0:T(4,128)S(1)} copy-done((f32[3,4,4,128]{3,2,1,0:T(4,128)S(1)}, f32[3,4,4,128]{3,2,1,0:T(4,128)}, u32[]{:S(2)}) %copy-start.4) | copy-done | bytes 24600
  3.9 1.0 %prep.1 = (f32[16,32,128]{2,1,0:T(8,128)S(1)}, f32[16,8,128]{2,1,0:T(8,128)S(1)}, f32[16,2,128]{2,1,0:T(2,128)S(1)}, f32[16,8,128]{2,1,0:T(8,128)S(1)}) custom-call(f32[256,128]{1,0:T(8,128)S(1)} %bitcast.12, f32[256,128]{1,0:T(8,128)S(1)} %bitcast.13, f32[64,128]{1,0:T(8,128)S(1)} %bitcast.16, f32[48,128]{1,0:T(8,128)S(1)} %bitcast.17), custom_call_target="tpu_custom_call" | custom-call | tf_op jit(solution)/shard_map/prep/pallas_call | solution.py:445
  4.9 21.3 %halo.1 = (f32[12,12,32,128]{3,2,1,0:T(8,128)S(1)}, f32[8,8,8,128]{3,2,1,0:T(8,128)S(1)}, f32[2,8,8,2,128]{4,3,2,1,0:T(2,128)S(1)}, f32[2,4,4,8,128]{4,3,2,1,0:T(8,128)S(1)}) custom-call(f32[4,4,32,128]{3,2,1,0:T(8,128)S(1)} %bitcast.10, f32[4,4,8,128]{3,2,1,0:T(8,128)S(1)} %bitcast.14, f32[4,4,2,128]{3,2,1,0:T(2,128)S(1)} %bitcast.18, ...), custom_call_target="tpu_custom_call" | custom-call | tf_op jit(solution)/shard_map/halo/pallas_call | solution.py:460
  26.3 26.1 %response.1 = (f32[4096,128]{1,0:T(8,128)}, f32[256,256]{1,0:T(8,128)S(1)}) custom-call(f32[12,12,32,128]{3,2,1,0:T(8,128)S(1)} %get-tuple-element.16.wide, f32[8,8,8,128]{3,2,1,0:T(8,128)S(1)} %get-tuple-element.17.wfld, f32[2,8,8,2,128]{4,3,2,1,0:T(2,128)S(1)} %get-tuple-element.18.wz, f32[2,4,4,8,128]{4,3,2,1,0:T(8,128)S(1)} %get-tuple-element.19.wg), custom_call_target="tpu_custom_call" | custom-call | tf_op jit(solution)/shard_map/response/pallas_call | solution.py:484
  52.4 0.0 copy-start
  52.4 0.7 %copy-done = f32[256,256]{1,0:T(8,128)} copy-done((f32[256,256]{1,0:T(8,128)}, f32[256,256]{1,0:T(8,128)S(1)}, u32[]{:S(2)}) %copy-start) | copy-done | bytes 262168
  53.1 12.0 %scatter.1 = f32[8,256]{1,0:T(8,128)} custom-call(f32[4,4,2,8,256]{4,3,2,1,0:T(8,128)} %bitcast.11), custom_call_target="tpu_custom_call" | custom-call | tf_op jit(solution)/shard_map/scatter/pallas_call | solution.py:515
  65.1 1.3 %copy.7 = f32[8,256]{1,0:T(8,128)} copy(f32[8,256]{1,0:T(8,128)} %scatter.1) | data formatting | bytes 16384
Async XLA Ops:
  0.6 0.9 %copy-start.1 = (f32[16,4,4,128]{3,2,1,0:T(4,128)S(1)}, f32[16,4,4,128]{3,2,1,0:T(4,128)}, u32[]{:S(2)}) copy-start(f32[16,4,4,128]{3,2,1,0:T(4,128)} %param.4) | copy-start | bytes 393220
  1.5 0.9 %copy-start.2 = (f32[16,4,4,128]{3,2,1,0:T(4,128)S(1)}, f32[16,4,4,128]{3,2,1,0:T(4,128)}, u32[]{:S(2)}) copy-start(f32[16,4,4,128]{3,2,1,0:T(4,128)} %param.5) | copy-start | bytes 393220
  2.4 0.8 %copy-start.3 = (f32[4,4,4,128]{3,2,1,0:T(4,128)S(1)}, f32[4,4,4,128]{3,2,1,0:T(4,128)}, u32[]{:S(2)}) copy-start(f32[4,4,4,128]{3,2,1,0:T(4,128)} %param.6) | copy-start | bytes 98308
  3.2 0.7 %copy-start.4 = (f32[3,4,4,128]{3,2,1,0:T(4,128)S(1)}, f32[3,4,4,128]{3,2,1,0:T(4,128)}, u32[]{:S(2)}) copy-start(f32[3,4,4,128]{3,2,1,0:T(4,128)} %param.7) | copy-start | bytes 73732
  52.4 0.7 %copy-start = (f32[256,256]{1,0:T(8,128)}, f32[256,256]{1,0:T(8,128)S(1)}, u32[]{:S(2)}) copy-start(f32[256,256]{1,0:T(8,128)S(1)} %get-tuple-element.21) | copy-start | bytes 786436
where the time goes:
time: 66.8 us; the launch traced here: 66.4 us
  Pallas kernels  60.5 us (91%)
  local copies, waits for them, and re-layouts  5.29 us (8%)
    pallas_call x1, Pallas kernels, on_device(): pl.pallas_call(functools.partial(main_kernel, (nocc, nvir)), grid=(nocc,)...  26.1 us
    pallas_call x1, Pallas kernels, on_device(): pl.pallas_call(halo_kernel, out_shape=(sds(bx + 8, by + 8, norb, lanes),...  21.3 us
    pallas_call x1, Pallas kernels, on_device(): pl.pallas_call(functools.partial(scatter_kernel, 1.0 / (cells * devices))...  12 us
    unnamed x11, local copies, waits for them, and re-layouts  5.29 us

commit v1 on v0

v1 whole, which is shorter than its diff:
```python
import functools

import jax
import jax.numpy as jnp
from jax import lax
from jax.experimental import pallas as pl
from jax.experimental.pallas import tpu as pltpu
from jax.sharding import PartitionSpec as P

MESH = pl.DeviceIdType.MESH
F32 = jnp.float32
BF16 = jnp.bfloat16
SHIFTS = (1, -1, 2, -2)
MIB = 1024 * 1024


def difference(f):
    return 8.0 * (f(1) - f(-1)) - (f(2) - f(-2))


def lanes_of(shape):
    return lax.broadcasted_iota(jnp.int32, shape, len(shape) - 1)


def edge_terms(gap, lane):
    axis = gap.ndim - 1
    lanes = gap.shape[axis]
    at = lane & 3
    two = jnp.where(at >= 2, -pltpu.roll(gap, lanes - 2, axis), pltpu.roll(gap, 2, axis))
    one = jnp.where(at == 3, pltpu.roll(gap, lanes - 1, axis), -pltpu.roll(gap, 1, axis))
    return two + jnp.where((at == 3) | (at == 0), 8.0 * one, 0.0)


def split(v):
    hi = v.astype(BF16)
    return hi, (v - hi.astype(F32)).astype(BF16)


def dot(a, b):
    return lax.dot_general(a, b, (((1,), (1,)), ((), ())), preferred_element_type=F32)


def flow_kernel(
    occ_in, vir_in, ker_in, grd_in,
    f0, f1, base, corr, cas,
    occ, vir, ker, grd, W, N, oS, vS, S0, S2, AL, C, A0, A1,
    pk, wz, pkn, px, py, E2, ez, L, S1a, S1b, Rha, Rla, Rhb, Rlb, LE, RE, RL,
    acc, part, got, acc2, got2,
    send, recv, own, send1, recv1, send2, recv2,
):
    nx, ny, nz = (lax.axis_size(a) for a in ("gx", "gy", "gz"))
    gx, gy, gz = (lax.axis_index(a) for a in ("gx", "gy", "gz"))
    bx, by = base.shape[0], base.shape[1]
    cells = bx * by
    lanes = occ.shape[1]
    half = lanes // 2
    nocc, nvir = occ.shape[0] // cells, vir.shape[0] // cells
    pairs = nocc * nvir
    rows_out = cas.shape[0]
    n_plane = nx * nz
    me = gx * nz + gz

    def plane(d):
        t = lax.rem(me + d, n_plane)
        tx, tz = t // nz, lax.rem(t, nz)
        return tx, tz, {"gx": tx, "gy": gy, "gz": tz}

    def column(d):
        t = lax.rem(gy + d, ny)
        return t, {"gx": gx, "gy": t, "gz": gz}

    def beside(axis, side):
        v, n = {"gx": (gx, nx), "gy": (gy, ny), "gz": (gz, nz)}[axis]
        where = {"gx": gx, "gy": gy, "gz": gz}
        where[axis] = lax.rem(v + 1, n) if side == 0 else lax.rem(v + n - 1, n)
        return where

    taken = [
        pltpu.make_async_copy(a, b, own.at[k])
        for k, (a, b) in enumerate(((occ_in, occ), (vir_in, vir), (ker_in, ker), (grd_in, grd)))
    ]
    for c in taken:
        c.start()
    barrier = pltpu.get_barrier_semaphore()
    for d in range(1, n_plane):
        pl.semaphore_signal(barrier, inc=1, device_id=plane(d)[2], device_id_type=MESH)
    for d in range(1, ny):
        pl.semaphore_signal(barrier, inc=1, device_id=column(d)[1], device_id_type=MESH)

    acc[...] = jnp.zeros_like(acc)
    for r in (Rhb, Rlb):
        r[...] = jnp.zeros_like(r)
    S1b[...] = jnp.zeros_like(S1b)
    L[0, 1] = jnp.zeros_like(L[0, 1])
    E2[...] = jnp.zeros_like(E2)
    lane = lanes_of((nvir, lanes))
    lane1 = lanes_of((1, lanes))
    at_edge = (lane < 2) | (lane >= lanes - 2)
    slot = lax.rem((lane + 2) // 4, lanes // 4)

    for c in taken:
        c.wait()
    packed = jnp.zeros((nocc, lanes), F32)
    for c in range(cells):
        x, y = divmod(c, by)
        o = occ[pl.ds(c, nocc, stride=cells), :]
        v = vir[pl.ds(c, nvir, stride=cells), :]
        W[x + 4, y + 4, 0:nocc] = o
        W[x + 4, y + 4, nocc:nocc + nvir] = v
        packed += pltpu.roll(jnp.where(at_edge, o, 0.0), 4 * c, 1)
        packed += pltpu.roll(jnp.where(at_edge, v, 0.0), 4 * c + half, 1)
        g = [grd[pl.ds(k * cells + c, 1), :] for k in range(3)]
        f = [ker[pl.ds(k * cells + c, 1), :] for k in range(4)]
        k1, k2, k3 = f[1] * (1.0 / 12.0), f[2] * (1.0 / 144.0), f[3] * (1.0 / 144.0)
        C[x, y] = jnp.concatenate(g + [k1, k2, k3, f[0], f[0]], axis=0)
        for m, ref in ((0, A0.at[x + 2, y]), (1, A1.at[x, y + 2])):
            q = k2 * g[m]
            a = [q * g[k] + k3 if k == m else q * g[k] for k in range(3)]
            ref[...] = jnp.concatenate(a + [k1 * g[m]], axis=0)
    pk[...] = packed
    pl.semaphore_wait(barrier, n_plane - 1 + ny - 1)

    copies = []

    def put(src, dst, device):
        k = len(copies)
        c = pltpu.make_async_remote_copy(
            src_ref=src, dst_ref=dst, send_sem=send.at[k], recv_sem=recv.at[k],
            device_id=device, device_id_type=MESH,
        )
        c.start()
        copies.append(c)
        return c

    in_x, in_y = pl.ds(4, bx), pl.ds(4, by)

    def near_src(b, side):
        return pl.ds(b + 2, 2) if side == 0 else pl.ds(4, 2)

    def near_dst(b, side):
        return pl.ds(2, 2) if side == 0 else pl.ds(b + 4, 2)

    def far_src(b, side):
        return pl.ds(b, 2) if side == 0 else pl.ds(6, 2)

    def far_dst(b, side):
        return pl.ds(0, 2) if side == 0 else pl.ds(b + 6, 2)

    def arm_src(b, side):
        return pl.ds(b, 2) if side == 0 else pl.ds(2, 2)

    def arm_dst(b, side):
        return pl.ds(0, 2) if side == 0 else pl.ds(b + 2, 2)

    zsides = range(1 if nz == 2 else 2)
    both = range(2)
    near_y = [
        put(W.at[in_x, near_src(by, s)], W.at[in_x, near_dst(by, s)], beside("gy", s)) for s in both
    ]
    z_in = [put(pk, wz.at[s], beside("gz", s)) for s in zsides]
    near_x = [
        put(W.at[near_src(bx, s), in_y], W.at[near_dst(bx, s), in_y], beside("gx", s)) for s in both
    ]
    arm_x = [put(A0.at[arm_src(bx, s)], A0.at[arm_dst(bx, s)], beside("gx", s)) for s in both]
    arm_y = [
        put(A1.at[:, arm_src(by, s)], A1.at[:, arm_dst(by, s)], beside("gy", s)) for s in both
    ]
    far_x = [
        put(W.at[far_src(bx, s), in_y], W.at[far_dst(bx, s), in_y], beside("gx", s)) for s in both
    ]
    far_y = [
        put(W.at[in_x, far_src(by, s)], W.at[in_x, far_dst(by, s)], beside("gy", s)) for s in both
    ]

    def multiply(count, place):
        def body(t, carry):
            x, y = place(t)
            v = W[x, y, nocc:nocc + nvir]
            for i in range(nocc):
                N[x, y, i] = W[x, y, i:i + 1] * v
            return carry

        lax.fori_loop(0, count, body, 0)

    def rim(t, b, lo, hi):
        return jnp.where(t < 2, t + lo, t + hi)

    multiply(cells, lambda t: (4 + t // by, 4 + lax.rem(t, by)))

    for c in z_in:
        c.wait_recv()
    low = (lanes_of((nocc, lanes)) & 3) < 2
    z_edges = wz[0] if nz == 2 else jnp.where(low, wz[1], wz[0])
    pkn[...] = z_edges
    turn_x = [put(pkn, px.at[s], beside("gx", s)) for s in both]
    turn_y = [put(pkn, py.at[s], beside("gy", s)) for s in both]

    def prepare(x, y, edges, c, fold):
        ao = pltpu.roll(edges, lax.rem(lanes - 4 * c, lanes), 1)
        av = pltpu.roll(edges, lax.rem(lanes + half - 4 * c, lanes), 1)
        o_own, v_own = W[x, y, 0:nocc], W[x, y, nocc:nocc + nvir]
        for k, s in enumerate(SHIFTS):
            m = lane < s if s > 0 else lane >= lanes + s
            scale = 8.0 if abs(s) == 1 else 1.0
            factor = scale if fold is None else scale * fold
            oS[k, x - 2, y - 2] = factor * pltpu.roll(jnp.where(m, ao, o_own), (-s) % lanes, 1)
            vS[k, x - 2, y - 2] = pltpu.roll(jnp.where(m, av, v_own), (-s) % lanes, 1)

    def prepare_center(t, carry):
        prepare(4 + t // by, 4 + lax.rem(t, by), pkn[...], t, None)
        return carry

    lax.fori_loop(0, cells, prepare_center, 0, unroll=2)

    own_o, own_v = pk[...], pltpu.roll(pk[...], half, 1)
    nb_o, nb_v = z_edges, pltpu.roll(z_edges, half, 1)
    for i in range(nocc):
        gap = nb_o[i:i + 1] * nb_v - own_o[i:i + 1] * own_v
        e = jnp.where(slot < cells, edge_terms(gap, lane), 0.0)
        hi, lo = split(e)
        LE[i * nvir:(i + 1) * nvir] = hi
        LE[pairs + i * nvir:pairs + (i + 1) * nvir] = lo

    for c in near_x:
        c.wait_recv()
    multiply(4 * by, lambda t: (rim(t // by, bx, 2, bx + 2), 4 + lax.rem(t, by)))

    def slope_z(x, y, i, shifted):
        p = [oS[k, x - 2, y - 2, i:i + 1] * shifted[k] for k in range(4)]
        return (p[0] - p[1]) - (p[2] - p[3])

    def first_pass(x, carry):
        for y in range(by):
            g0, g2 = C[x, y, 0:1], C[x, y, 2:3]
            shifted = [vS[k, x + 2, y + 2] for k in range(4)]
            h, at = y // 2, (y % 2) * 2 * lanes
            for i in range(nocc):
                r = i * nvir
                n = N[x + 4, y + 4, i]
                hi, lo = split(n)
                L[x, h, r:r + nvir, at:at + lanes] = hi
                L[x, h, pairs + r:pairs + r + nvir, at:at + lanes] = lo
                s2 = slope_z(x + 4, y + 4, i, shifted)
                S2[x, y, i] = s2
                s0 = difference(lambda t: N[x + 4 + t, y + 4, i])
                S0[x, y, i] = s0
                hi, lo = split(s0)
                L[x, h, r:r + nvir, at + lanes:at + 2 * lanes] = hi
                L[x, h, pairs + r:pairs + r + nvir, at + lanes:at + 2 * lanes] = lo
                AL[x, y, i] = g0 * s0 + g2 * s2
        return carry

    lax.fori_loop(0, bx, first_pass, 0)

    for c in turn_x + arm_x:
        c.wait_recv()

    def prepare_x(t, carry):
        k, y = t // by, lax.rem(t, by)
        side = k // 2
        c = jnp.where(k < 2, k + bx - 2, k - 2) * by + y
        a = rim(k, bx, 0, bx)
        prepare(a + 2, 4 + y, px[side], c, A0[a, y, 2:3])
        return carry

    lax.fori_loop(0, 4 * by, prepare_x, 0, unroll=2)

    for c in near_y:
        c.wait_recv()
    corner = [
        put(
            W.at[near_src(bx, sx), near_dst(by, sy)],
            W.at[near_dst(bx, sx), near_dst(by, sy)],
            beside("gx", sx),
        )
        for sy in both
        for sx in both
    ]
    multiply(4 * bx, lambda t: (4 + t // 4, rim(lax.rem(t, 4), by, 2, by + 2)))

    def second_pass_cell(x, y, S1, Rh, Rl):
        g0, g1, g2, k1, k2, k3, kk = (C[x, y, k:k + 1] for k in range(7))
        at, at1 = (y % 2) * 2 * lanes, (y % 2) * lanes
        c = x * by + y
        for i in range(nocc):
            r = i * nvir
            n = N[x + 4, y + 4, i]
            s1 = difference(lambda t: N[x + 4, y + 4 + t, i])
            al = AL[x, y, i] + g1 * s1
            sc = k1 * n + k2 * al
            fl0 = sc * g0 + k3 * S0[x, y, i]
            fl1 = sc * g1 + k3 * s1
            fl2 = sc * g2 + k3 * S2[x, y, i]
            f0[x + 2, y, i] = fl0
            f1[x, y + 2, i] = fl1
            turned = difference(lambda t: pltpu.roll(fl2, (-t) % lanes, 1))
            b = (kk * n + k1 * al) - turned
            base[x, y, i] = b
            deep = 4 * c + half * (2 * i // nocc)
            s = c + cells * (2 * i // nocc)
            j = i % (nocc // 2)
            E2[j] = jnp.where(slot == s, pltpu.roll(fl2, deep, 1), E2[j])
            hi, lo = split(s1)
            S1[r:r + nvir, at1:at1 + lanes] = hi
            S1[pairs + r:pairs + r + nvir, at1:at1 + lanes] = lo
            for v, to in ((b, at), (fl0, at + lanes), (fl1, 4 * lanes + at1)):
                hi, lo = split(v)
                Rh[r:r + nvir, to:to + lanes] = hi
                Rl[r:r + nvir, to:to + lanes] = lo

    def gather(left, S1, Rh, Rl):
        k = 4 * lanes
        top = dot(left[...], Rh[:, 0:k]) + dot(S1[...], Rh[:, k:k + 2 * lanes])
        low_part = dot(left[0:pairs], Rl[:, 0:k]) + dot(S1[0:pairs], Rl[:, k:k + 2 * lanes])
        acc[...] += (top[0:pairs] + top[pairs:]) + low_part

    def second_pass(x, carry):
        gather(L.at[jnp.maximum(x - 1, 0), 1], S1b, Rhb, Rlb)
        for y in range(0, 2):
            second_pass_cell(x, y, S1a, Rha, Rla)
        gather(L.at[x, 0], S1a, Rha, Rla)
        for y in range(2, 4):
            second_pass_cell(x, y, S1b, Rhb, Rlb)
        return carry

    lax.fori_loop(0, bx, second_pass, 0)
    z_out = [put(E2, ez.at[s], beside("gz", s)) for s in zsides]
    gather(L.at[bx - 1, 1], S1b, Rhb, Rlb)
    for i in range(nocc):
        e = E2[i % (nocc // 2)]
        if 2 * i >= nocc:
            e = pltpu.roll(e, half, 1)
        hi, lo = split(e)
        RE[i * nvir:(i + 1) * nvir] = hi
        RL[i * nvir:(i + 1) * nvir] = lo
    ends = dot(LE[...], RE[...])
    total = acc[...] + (ends[0:pairs] + ends[pairs:]) + dot(LE[0:pairs], RL[...])
    for tx in range(nx):
        for ty in range(ny):
            for tz in range(nz):
                r = ((tx * ny + ty) * nz + tz) * rows_out
                part[tx, ty, tz] = total[r:r + rows_out]
    first = []
    for d in range(1, n_plane):
        tx, tz, target = plane(d)
        c = pltpu.make_async_remote_copy(
            src_ref=part.at[tx, :, tz], dst_ref=got.at[d],
            send_sem=send1.at[d], recv_sem=recv1.at[d],
            device_id=target, device_id_type=MESH,
        )
        c.start()
        first.append(c)

    def arm_pass(count, place, A, out):
        def body(t, carry):
            x, y, a, b = place(t)
            shifted = [vS[k, x - 2, y - 2] for k in range(4)]
            c0, c1, c3 = A[a, b, 0:1], A[a, b, 1:2], A[a, b, 3:4]
            for i in range(nocc):
                s0 = difference(lambda t: N[x + t, y, i])
                s1 = difference(lambda t: N[x, y + t, i])
                out[a, b, i] = (c0 * s0 + c1 * s1) + (slope_z(x, y, i, shifted) + c3 * N[x, y, i])
            return carry

        lax.fori_loop(0, count, body, 0)

    for c in far_x + corner:
        c.wait_recv()
    multiply(4 * by, lambda t: (rim(t // by, bx, 0, bx + 4), 4 + lax.rem(t, by)))
    multiply(16, lambda t: (rim(t // 4, bx, 2, bx + 2), rim(lax.rem(t, 4), by, 2, by + 2)))

    def at_x(t):
        a, y = rim(t // by, bx, 0, bx), lax.rem(t, by)
        return a + 2, y + 4, a, y

    arm_pass(4 * by, at_x, A0, f0)

    for c in turn_y + arm_y:
        c.wait_recv()

    def prepare_y(t, carry):
        x, k = t // 4, lax.rem(t, 4)
        side = k // 2
        c = x * by + jnp.where(k < 2, k + by - 2, k - 2)
        b = rim(k, by, 0, by)
        prepare(4 + x, b + 2, py[side], c, A1[x, b, 2:3])
        return carry

    lax.fori_loop(0, 4 * bx, prepare_y, 0, unroll=2)

    mine = part[gx, :, gz]
    for d, c in enumerate(first):
        c.wait_recv()
        mine = mine + got[d + 1]
    acc2[...] = mine

    for c in far_y:
        c.wait_recv()
    multiply(4 * bx, lambda t: (4 + t // 4, rim(lax.rem(t, 4), by, 0, by + 4)))

    second = []
    for d in range(1, ny):
        t, target = column(d)
        c = pltpu.make_async_remote_copy(
            src_ref=acc2.at[t], dst_ref=got2.at[d],
            send_sem=send2.at[d], recv_sem=recv2.at[d],
            device_id=target, device_id_type=MESH,
        )
        c.start()
        second.append(c)

    def at_y(t):
        x, b = t // 4, rim(lax.rem(t, 4), by, 0, by)
        return x + 4, b + 2, x, b

    arm_pass(4 * bx, at_y, A1, f1)

    for c in z_out:
        c.wait_recv()
    for j in range(nocc // 2):
        outer = ez[0, j] if nz == 2 else jnp.where((lane & 3) < 2, ez[1, j], ez[0, j])
        corr[j] = edge_terms(outer - E2[j], lane)
    for c in copies + first + second:
        c.wait_send()
    mine = acc2[gy]
    for d, c in enumerate(second):
        c.wait_recv()
        mine = mine + got2[d + 1]
    cas[...] = mine * (1.0 / (cells * lanes * nx * ny * nz))


def finish_kernel(f0, f1, base, corr, cas_in, pot_out, cas, pot, sem):
    bx, by, nocc, nvir, lanes = base.shape
    cells = bx * by
    half = lanes // 2
    cas[...] = cas_in[...]
    lane = lanes_of((nvir, lanes))
    at_edge = (lane < 2) | (lane >= lanes - 2)
    rows = nvir * cells

    def body(i, carry):
        deep = i // (nocc // 2)
        e = corr[lax.rem(i, nocc // 2)]
        row0 = pl.multiple_of(i * rows, rows)
        for y in range(by):
            a = [f0[x, y, i] for x in range(bx + 4)]
            for x in range(bx):
                c = x * by + y
                b = [f1[x, y + k, i] for k in (0, 1, 3, 4)]
                inner = (a[x + 3] - a[x + 1]) + (b[2] - b[1])
                outer = (a[x + 4] - a[x]) + (b[3] - b[0])
                turned = pltpu.roll(e, lax.rem(2 * lanes - 4 * c - half * deep, lanes), 1)
                v = base[x, y, i] - (8.0 * inner - outer)
                pot[pl.ds(row0 + c, nvir, stride=cells), :] = v - jnp.where(at_edge, turned, 0.0)
        pltpu.make_async_copy(pot.at[pl.ds(row0, rows)], pot_out.at[pl.ds(row0, rows)], sem.at[i]).start()
        return carry

    lax.fori_loop(0, nocc, body, 0)
    for i in range(nocc):
        block = pl.ds(i * rows, rows)
        pltpu.make_async_copy(pot.at[block], pot_out.at[block], sem.at[i]).wait()


def on_device(occupied, virtual, kernel_fields, density_grad):
    nocc, bx, by, lanes = occupied.shape
    nvir = virtual.shape[0]
    nx, ny, nz = (lax.axis_size(a) for a in ("gx", "gy", "gz"))
    devices = nx * ny * nz
    cells = bx * by
    pairs = nocc * nvir
    norb = nocc + nvir
    rows = pairs // devices
    sds = lambda *s: jax.ShapeDtypeStruct(s, F32)
    v32 = lambda *s: pltpu.VMEM(s, F32)
    v16 = lambda *s: pltpu.VMEM(s, BF16)
    dma = lambda n: pltpu.SemaphoreType.DMA((n,))
    vmem = pl.BlockSpec(memory_space=pltpu.VMEM)
    hbm = pl.BlockSpec(memory_space=pltpu.HBM)
    zs = 1 if nz == 2 else 2
    flat = lambda a: a.reshape(-1, lanes)
    outs = pl.pallas_call(
        flow_kernel,
        out_shape=(
            sds(bx + 4, by, nocc, nvir, lanes),
            sds(bx, by + 4, nocc, nvir, lanes),
            sds(bx, by, nocc, nvir, lanes),
            sds(nocc // 2, nvir, lanes),
            sds(rows, pairs),
        ),
        in_specs=[hbm] * 4,
        out_specs=[vmem] * 5,
        scratch_shapes=[
            v32(nocc * cells, lanes), v32(nvir * cells, lanes), v32(4 * cells, lanes), v32(3 * cells, lanes),
            v32(bx + 8, by + 8, norb, lanes),
            v32(bx + 8, by + 8, nocc, nvir, lanes),
            v32(4, bx + 4, by + 4, nocc, lanes),
            v32(4, bx + 4, by + 4, nvir, lanes),
            v32(bx, by, nocc, nvir, lanes), v32(bx, by, nocc, nvir, lanes), v32(bx, by, nocc, nvir, lanes),
            v32(bx, by, 8, lanes), v32(bx + 4, by, 4, lanes), v32(bx, by + 4, 4, lanes),
            v32(nocc, lanes), v32(zs, nocc, lanes), v32(nocc, lanes), v32(2, nocc, lanes), v32(2, nocc, lanes),
            v32(nocc // 2, nvir, lanes), v32(zs, nocc // 2, nvir, lanes),
            v16(bx, 2, 2 * pairs, 4 * lanes),
            v16(2 * pairs, 2 * lanes), v16(2 * pairs, 2 * lanes),
            v16(pairs, 6 * lanes), v16(pairs, 6 * lanes), v16(pairs, 6 * lanes), v16(pairs, 6 * lanes),
            v16(2 * pairs, lanes), v16(pairs, lanes), v16(pairs, lanes),
            v32(pairs, pairs),
            v32(nx, ny, nz, rows, pairs),
            v32(nx * nz, ny, rows, pairs),
            v32(ny, rows, pairs), v32(ny, rows, pairs),
            dma(28), dma(28), dma(4), dma(nx * nz), dma(nx * nz), dma(ny), dma(ny),
        ],
        compiler_params=pltpu.CompilerParams(
            collective_id=0, has_side_effects=True, vmem_limit_bytes=46 * MIB
        ),
        name="flow",
    )(flat(occupied), flat(virtual), flat(kernel_fields), flat(density_grad))
    pot, casida = pl.pallas_call(
        finish_kernel,
        out_shape=(sds(pairs * cells, lanes), sds(rows, pairs)),
        in_specs=[vmem] * 5,
        out_specs=(hbm, vmem),
        scratch_shapes=[v32(pairs * cells, lanes), dma(nocc)],
        compiler_params=pltpu.CompilerParams(vmem_limit_bytes=4 * MIB),
        name="finish",
    )(*outs)
    return pot.reshape(pairs, bx, by, lanes), casida


def solution(mesh):
    spec = P(None, "gx", "gy", "gz")
    return jax.shard_map(
        on_device,
        mesh=mesh,
        in_specs=(spec,) * 4,
        out_specs=(spec, P(("gx", "gy", "gz"), None)),
        check_vma=False,
    )
```

time: 66.8 us -> 42.7 us (0.64)
  Pallas kernels: 60.5 us -> 36.2 us
    pallas_call x4 -> x2, Pallas kernels: 60.5 us -> 36.2 us  [the longest x1 32.8 us: on_device(): pl.pallas_call(flow_kernel, out_shape=(sds(bx + 4, by, nocc, nvir, lanes)...]
    unnamed x11 -> x10, local copies, waits for them, and re-layouts: 5.29 us -> 5.48 us
where the time goes in v1:
time: 42.7 us; the launch traced here: 42.4 us
  Pallas kernels  36.2 us (85%)
  local copies, waits for them, and re-layouts  5.48 us (13%)
  between operations  0.66 us (2%)
    pallas_call x1, Pallas kernels, on_device(): pl.pallas_call(flow_kernel, out_shape=(sds(bx + 4, by, nocc, nvir, lanes)...  32.8 us
    unnamed x10, local copies, waits for them, and re-layouts  5.48 us
    pallas_call x1, Pallas kernels, on_device(): pl.pallas_call(finish_kernel, out_shape=(sds(pairs * cells, lanes), sds(r...  3.42 us

profile of v1, /device:TPU:0, one launch (start us, length us, event | category | flops | bytes accessed | tf_op | source)
XLA Modules:
  0.0 42.4 jit_solution(15305836574765785839)
XLA Ops:
  0.6 0.0 copy-start.1
  0.6 0.9 %copy-done.1 = f32[16,4,4,128]{3,2,1,0:T(4,128)S(1)} copy-done((f32[16,4,4,128]{3,2,1,0:T(4,128)S(1)}, f32[16,4,4,128]{3,2,1,0:T(4,128)}, u32[]{:S(2)}) %copy-start.1) | copy-done | bytes 131096
  1.5 0.0 copy-start.2
  1.5 0.9 %copy-done.2 = f32[16,4,4,128]{3,2,1,0:T(4,128)S(1)} copy-done((f32[16,4,4,128]{3,2,1,0:T(4,128)S(1)}, f32[16,4,4,128]{3,2,1,0:T(4,128)}, u32[]{:S(2)}) %copy-start.2) | copy-done | bytes 131096
  2.4 0.0 copy-start.3
  2.4 0.8 %copy-done.3 = f32[4,4,4,128]{3,2,1,0:T(4,128)S(1)} copy-done((f32[4,4,4,128]{3,2,1,0:T(4,128)S(1)}, f32[4,4,4,128]{3,2,1,0:T(4,128)}, u32[]{:S(2)}) %copy-start.3) | copy-done | bytes 32792
  3.2 0.0 copy-start.4
  3.2 0.7 %copy-done.4 = f32[3,4,4,128]{3,2,1,0:T(4,128)S(1)} copy-done((f32[3,4,4,128]{3,2,1,0:T(4,128)S(1)}, f32[3,4,4,128]{3,2,1,0:T(4,128)}, u32[]{:S(2)}) %copy-start.4) | copy-done | bytes 24600
  3.9 32.8 %flow.1 = (f32[8,4,16,16,128]{4,3,2,1,0:T(8,128)S(1)}, f32[4,8,16,16,128]{4,3,2,1,0:T(8,128)}, f32[4,4,16,16,128]{4,3,2,1,0:T(8,128)S(1)}, f32[8,16,128]{2,1,0:T(8,128)S(1)}, f32[8,256]{1,0:T(8,128)S(1)}) custom-call(f32[256,128]{1,0:T(8,128)S(1)} %bitcast.5, f32[256,128]{1,0:T(8,128)S(1)} %bitcast.6, f32[64,128]{1,0:T(8,128)S(1)} %bitcast.7, ...), custom_call_target="tpu_custom_call" | custom-call | tf_op jit(solution)/shard_map/flow/pallas_call | solution.py:481
  36.8 0.0 copy-start
  36.8 2.2 %copy-done = f32[4,8,16,16,128]{4,3,2,1,0:T(8,128)S(1)} copy-done((f32[4,8,16,16,128]{4,3,2,1,0:T(8,128)S(1)}, f32[4,8,16,16,128]{4,3,2,1,0:T(8,128)}, u32[]{:S(2)}) %copy-start) | copy-done | bytes 4194328
  39.0 3.4 %finish.1 = (f32[4096,128]{1,0:T(8,128)}, f32[8,256]{1,0:T(8,128)}) custom-call(f32[8,4,16,16,128]{4,3,2,1,0:T(8,128)S(1)} %get-tuple-element.9.f0, f32[4,8,16,16,128]{4,3,2,1,0:T(8,128)S(1)} %copy-done, f32[4,4,16,16,128]{4,3,2,1,0:T(8,128)S(1)} %get-tuple-element.11.base, f32[8,16,128]{2,1,0:T(8,128)S(1)} %get-tuple-element.12.corr, ...), custom_call_target="tpu_custom_call" | custom-call | tf_op jit(solution)/shard_map/finish/pallas_call | solution.py:517
Async XLA Ops:
  0.6 0.9 %copy-start.1 = (f32[16,4,4,128]{3,2,1,0:T(4,128)S(1)}, f32[16,4,4,128]{3,2,1,0:T(4,128)}, u32[]{:S(2)}) copy-start(f32[16,4,4,128]{3,2,1,0:T(4,128)} %param.4) | copy-start | bytes 393220
  1.5 0.9 %copy-start.2 = (f32[16,4,4,128]{3,2,1,0:T(4,128)S(1)}, f32[16,4,4,128]{3,2,1,0:T(4,128)}, u32[]{:S(2)}) copy-start(f32[16,4,4,128]{3,2,1,0:T(4,128)} %param.5) | copy-start | bytes 393220
  2.4 0.8 %copy-start.3 = (f32[4,4,4,128]{3,2,1,0:T(4,128)S(1)}, f32[4,4,4,128]{3,2,1,0:T(4,128)}, u32[]{:S(2)}) copy-start(f32[4,4,4,128]{3,2,1,0:T(4,128)} %param.6) | copy-start | bytes 98308
  3.2 0.7 %copy-start.4 = (f32[3,4,4,128]{3,2,1,0:T(4,128)S(1)}, f32[3,4,4,128]{3,2,1,0:T(4,128)}, u32[]{:S(2)}) copy-start(f32[3,4,4,128]{3,2,1,0:T(4,128)} %param.7) | copy-start | bytes 73732
  36.8 2.2 %copy-start = (f32[4,8,16,16,128]{4,3,2,1,0:T(8,128)S(1)}, f32[4,8,16,16,128]{4,3,2,1,0:T(8,128)}, u32[]{:S(2)}) copy-start(f32[4,8,16,16,128]{4,3,2,1,0:T(8,128)} %get-tuple-element.10.f1) | copy-start | bytes 12582916

commit v2 on v1

--- a/solution.py
+++ b/solution.py
@@ -510,10 +510,10 @@
             dma(28), dma(28), dma(4), dma(nx * nz), dma(nx * nz), dma(ny), dma(ny),
         ],
         compiler_params=pltpu.CompilerParams(
-            collective_id=0, has_side_effects=True, vmem_limit_bytes=46 * MIB
+            collective_id=0, has_side_effects=True, vmem_limit_bytes=42 * MIB
         ),
         name="flow",
-    )(flat(occupied), flat(virtual), flat(kernel_fields), flat(density_grad))
+    )(*(pltpu.with_memory_space_constraint(flat(a), pltpu.HBM) for a in (occupied, virtual, kernel_fields, density_grad)))
     pot, casida = pl.pallas_call(
         finish_kernel,
         out_shape=(sds(pairs * cells, lanes), sds(rows, pairs)),

time: 42.7 us -> 35.1 us (0.82)
  local copies, waits for them, and re-layouts: 5.48 us -> 0 us
  Pallas kernels: 36.2 us -> 34.3 us
    unnamed x10 -> x0, local copies, waits for them, and re-layouts: 5.48 us -> none
    pallas_call x1, Pallas kernels: 32.8 us -> 30.8 us  [on_device(): pl.pallas_call(flow_kernel, out_shape=(sds(bx + 4, by, nocc, nvir, lanes)...]
where the time goes in v2:
time: 35.1 us; the launch traced here: 34.9 us
  Pallas kernels  34.3 us (98%)
  between operations  0.64 us (2%)
    pallas_call x1, Pallas kernels, on_device(): pl.pallas_call(flow_kernel, out_shape=(sds(bx + 4, by, nocc, nvir, lanes)...  30.8 us
    pallas_call x1, Pallas kernels, on_device(): pl.pallas_call(finish_kernel, out_shape=(sds(pairs * cells, lanes), sds(r...  3.45 us

profile of v2, /device:TPU:0, one launch (start us, length us, event | category | flops | bytes accessed | tf_op | source)
XLA Modules:
  0.0 34.9 jit_solution(9043670122721587313)
XLA Ops:
  0.6 30.8 %flow.1 = (f32[8,4,16,16,128]{4,3,2,1,0:T(8,128)S(1)}, f32[4,8,16,16,128]{4,3,2,1,0:T(8,128)S(1)}, f32[4,4,16,16,128]{4,3,2,1,0:T(8,128)S(1)}, f32[8,16,128]{2,1,0:T(8,128)S(1)}, f32[8,256]{1,0:T(8,128)S(1)}) custom-call(f32[256,128]{1,0:T(8,128)} %bitcast.5, f32[256,128]{1,0:T(8,128)} %bitcast.6, f32[64,128]{1,0:T(8,128)} %bitcast.7, f32[48,128]{1,0:T(8,128)} %bitcast.8), custom_call_target="tpu_custom_call" | custom-call | tf_op jit(solution)/shard_map/flow/pallas_call | solution.py:481
  31.5 3.4 %finish.1 = (f32[4096,128]{1,0:T(8,128)}, f32[8,256]{1,0:T(8,128)}) custom-call(f32[8,4,16,16,128]{4,3,2,1,0:T(8,128)S(1)} %get-tuple-element.9.f0, f32[4,8,16,16,128]{4,3,2,1,0:T(8,128)S(1)} %get-tuple-element.10.f1, f32[4,4,16,16,128]{4,3,2,1,0:T(8,128)S(1)} %get-tuple-element.11.base, f32[8,16,128]{2,1,0:T(8,128)S(1)} %get-tuple-element.12.corr, ...), custom_call_target="tpu_custom_call" | custom-call | tf_op jit(solution)/shard_map/finish/pallas_call | solution.py:517

commit v3 on v2

v3 whole, which is shorter than its diff:
```python
import functools

import jax
import jax.numpy as jnp
from jax import lax
from jax.experimental import pallas as pl
from jax.experimental.pallas import tpu as pltpu
from jax.sharding import PartitionSpec as P

MESH = pl.DeviceIdType.MESH
F32 = jnp.float32
BF16 = jnp.bfloat16
SHIFTS = (1, -1, 2, -2)
MIB = 1024 * 1024


def difference(f):
    return 8.0 * (f(1) - f(-1)) - (f(2) - f(-2))


def lanes_of(shape):
    return lax.broadcasted_iota(jnp.int32, shape, len(shape) - 1)


def edge_terms(gap, lane):
    axis = gap.ndim - 1
    lanes = gap.shape[axis]
    at = lane & 3
    two = jnp.where(at >= 2, -pltpu.roll(gap, lanes - 2, axis), pltpu.roll(gap, 2, axis))
    one = jnp.where(at == 3, pltpu.roll(gap, lanes - 1, axis), -pltpu.roll(gap, 1, axis))
    return two + jnp.where((at == 3) | (at == 0), 8.0 * one, 0.0)


def rest(v):
    return v - v.astype(BF16).astype(F32)


def dot(a, b):
    return lax.dot_general(a, b, (((1,), (1,)), ((), ())), preferred_element_type=F32)


def flow_kernel(
    occ_in, vir_in, ker_in, grd_in,
    pot, cas,
    occ, vir, ker, grd, W, N, oS, vS, S0, S1, S2, AL, NL, S0L, LO, f0, f1, base, C, A0, A1,
    pk, wz, pkn, px, py, E2, ez, corr, LE, LEL,
    acc, part, got, acc2, got2,
    send, recv, own, send1, recv1, send2, recv2,
):
    nx, ny, nz = (lax.axis_size(a) for a in ("gx", "gy", "gz"))
    gx, gy, gz = (lax.axis_index(a) for a in ("gx", "gy", "gz"))
    bx, by = base.shape[0], base.shape[1]
    cells = bx * by
    lanes = occ.shape[1]
    half = lanes // 2
    nocc, nvir = occ.shape[0] // cells, vir.shape[0] // cells
    pairs = nocc * nvir
    rows_out = cas.shape[0]
    n_plane = nx * nz
    me = gx * nz + gz

    def plane(d):
        t = lax.rem(me + d, n_plane)
        tx, tz = t // nz, lax.rem(t, nz)
        return tx, tz, {"gx": tx, "gy": gy, "gz": tz}

    def column(d):
        t = lax.rem(gy + d, ny)
        return t, {"gx": gx, "gy": t, "gz": gz}

    def beside(axis, side):
        v, n = {"gx": (gx, nx), "gy": (gy, ny), "gz": (gz, nz)}[axis]
        where = {"gx": gx, "gy": gy, "gz": gz}
        where[axis] = lax.rem(v + 1, n) if side == 0 else lax.rem(v + n - 1, n)
        return where

    taken = [
        pltpu.make_async_copy(a, b, own.at[k])
        for k, (a, b) in enumerate(((occ_in, occ), (vir_in, vir), (ker_in, ker), (grd_in, grd)))
    ]
    for c in taken:
        c.start()
    barrier = pltpu.get_barrier_semaphore()
    for d in range(1, n_plane):
        pl.semaphore_signal(barrier, inc=1, device_id=plane(d)[2], device_id_type=MESH)
    for d in range(1, ny):
        pl.semaphore_signal(barrier, inc=1, device_id=column(d)[1], device_id_type=MESH)

    E2[...] = jnp.zeros_like(E2)
    lane = lanes_of((nvir, lanes))
    at_edge = (lane < 2) | (lane >= lanes - 2)
    slot = lax.rem((lane + 2) // 4, lanes // 4)

    def own_rows(c):
        x, y = divmod(c, by)
        o = occ[pl.ds(c, nocc, stride=cells), :]
        v = vir[pl.ds(c, nvir, stride=cells), :]
        return x, y, o, v

    taken[0].wait()
    taken[1].wait()
    for c in range(cells):
        x, y, o, v = own_rows(c)
        W[x + 4, y + 4, 0:nocc] = o
        W[x + 4, y + 4, nocc:nocc + nvir] = v
    pl.semaphore_wait(barrier, n_plane - 1 + ny - 1)

    copies = []

    def put(src, dst, device):
        k = len(copies)
        c = pltpu.make_async_remote_copy(
            src_ref=src, dst_ref=dst, send_sem=send.at[k], recv_sem=recv.at[k],
            device_id=device, device_id_type=MESH,
        )
        c.start()
        copies.append(c)
        return c

    in_x, in_y = pl.ds(4, bx), pl.ds(4, by)

    def near_src(b, side):
        return pl.ds(b + 2, 2) if side == 0 else pl.ds(4, 2)

    def near_dst(b, side):
        return pl.ds(2, 2) if side == 0 else pl.ds(b + 4, 2)

    def layer_src(b, side, depth):
        return pl.ds(b + 4 - depth, 1) if side == 0 else pl.ds(3 + depth, 1)

    def layer_dst(b, side, depth):
        return pl.ds(4 - depth, 1) if side == 0 else pl.ds(b + 3 + depth, 1)

    def far_src(b, side):
        return pl.ds(b, 2) if side == 0 else pl.ds(6, 2)

    def far_dst(b, side):
        return pl.ds(0, 2) if side == 0 else pl.ds(b + 6, 2)

    def arm_src(b, side):
        return pl.ds(b, 2) if side == 0 else pl.ds(2, 2)

    def arm_dst(b, side):
        return pl.ds(0, 2) if side == 0 else pl.ds(b + 2, 2)

    zsides = range(1 if nz == 2 else 2)
    both = range(2)
    near_y = [
        [
            put(
                W.at[in_x, layer_src(by, s, depth)],
                W.at[in_x, layer_dst(by, s, depth)],
                beside("gy", s),
            )
            for s in both
        ]
        for depth in (1, 2)
    ]
    near_x = [
        put(W.at[near_src(bx, s), in_y], W.at[near_dst(bx, s), in_y], beside("gx", s)) for s in both
    ]
    taken[2].wait()
    taken[3].wait()
    packed = jnp.zeros((nocc, lanes), F32)
    for c in range(cells):
        x, y, o, v = own_rows(c)
        packed += pltpu.roll(jnp.where(at_edge, o, 0.0), 4 * c, 1)
        packed += pltpu.roll(jnp.where(at_edge, v, 0.0), 4 * c + half, 1)
        g = [grd[pl.ds(k * cells + c, 1), :] for k in range(3)]
        f = [ker[pl.ds(k * cells + c, 1), :] for k in range(4)]
        k1, k2, k3 = f[1] * (1.0 / 12.0), f[2] * (1.0 / 144.0), f[3] * (1.0 / 144.0)
        C[x, y] = jnp.concatenate(g + [k1, k2, k3, f[0], f[0]], axis=0)
        for m, ref in ((0, A0.at[x + 2, y]), (1, A1.at[x, y + 2])):
            q = k2 * g[m]
            a = [q * g[k] + k3 if k == m else q * g[k] for k in range(3)]
            ref[...] = jnp.concatenate(a + [k1 * g[m]], axis=0)
    pk[...] = packed
    z_in = [put(pk, wz.at[s], beside("gz", s)) for s in zsides]
    arm_x = [put(A0.at[arm_src(bx, s)], A0.at[arm_dst(bx, s)], beside("gx", s)) for s in both]
    arm_y = [
        put(A1.at[:, arm_src(by, s)], A1.at[:, arm_dst(by, s)], beside("gy", s)) for s in both
    ]

    def multiply(count, place, unroll=2):
        def body(t, carry):
            x, y = place(t)
            v = W[x, y, nocc:nocc + nvir]
            for i in range(nocc):
                N[x, y - 2, i] = W[x, y, i:i + 1] * v
            return carry

        lax.fori_loop(0, count, body, 0, unroll=unroll)

    def rim(t, b, lo, hi):
        return jnp.where(t < 2, t + lo, t + hi)

    multiply(cells, lambda t: (4 + t // by, 4 + lax.rem(t, by)))

    for c in z_in:
        c.wait_recv()
    low = (lanes_of((nocc, lanes)) & 3) < 2
    z_edges = wz[0] if nz == 2 else jnp.where(low, wz[1], wz[0])
    pkn[...] = z_edges
    turn_x = [put(pkn, px.at[s], beside("gx", s)) for s in both]
    turn_y = [put(pkn, py.at[s], beside("gy", s)) for s in both]
    far_x = [
        put(W.at[far_src(bx, s), in_y], W.at[far_dst(bx, s), in_y], beside("gx", s)) for s in both
    ]
    far_y = [
        put(W.at[in_x, far_src(by, s)], W.at[in_x, far_dst(by, s)], beside("gy", s)) for s in both
    ]

    def prepare(x, y, edges, c, fold):
        ao = pltpu.roll(edges, lax.rem(lanes - 4 * c, lanes), 1)
        av = pltpu.roll(edges, lax.rem(lanes + half - 4 * c, lanes), 1)
        o_own, v_own = W[x, y, 0:nocc], W[x, y, nocc:nocc + nvir]
        for k, s in enumerate(SHIFTS):
            m = lane < s if s > 0 else lane >= lanes + s
            scale = 8.0 if abs(s) == 1 else 1.0
            factor = scale if fold is None else scale * fold
            oS[k, x - 2, y - 2] = factor * pltpu.roll(jnp.where(m, ao, o_own), (-s) % lanes, 1)
            vS[k, x - 2, y - 2] = pltpu.roll(jnp.where(m, av, v_own), (-s) % lanes, 1)

    def prepare_center(t, carry):
        prepare(4 + t // by, 4 + lax.rem(t, by), pkn[...], t, None)
        return carry

    lax.fori_loop(0, cells, prepare_center, 0, unroll=4)

    own_o, own_v = pk[...], pltpu.roll(pk[...], half, 1)
    nb_o, nb_v = z_edges, pltpu.roll(z_edges, half, 1)
    for i in range(nocc):
        gap = nb_o[i:i + 1] * nb_v - own_o[i:i + 1] * own_v
        e = jnp.where(slot < cells, edge_terms(gap, lane), 0.0)
        LE[i] = e
        LEL[i] = rest(e)

    for c in near_x:
        c.wait_recv()
    multiply(4 * by, lambda t: (rim(t // by, bx, 2, bx + 2), 4 + lax.rem(t, by)))

    def slope_z(x, y, i, shifted):
        p = [oS[k, x + 2, y + 2, i:i + 1] * shifted[k] for k in range(4)]
        return (p[0] - p[1]) - (p[2] - p[3])

    def n_at(x, y, i):
        return N[x + 4, y + 2, i]

    def first_pass(x, carry):
        for y in range(by):
            g0, g2 = C[x, y, 0:1], C[x, y, 2:3]
            shifted = [vS[k, x + 2, y + 2] for k in range(4)]
            for i in range(nocc):
                NL[x, y, i] = rest(n_at(x, y, i))
                s2 = slope_z(x, y, i, shifted)
                S2[x, y, i] = s2
                s0 = difference(lambda t: n_at(x + t, y, i))
                S0[x, y, i] = s0
                S0L[x, y, i] = rest(s0)
                AL[x, y, i] = g0 * s0 + g2 * s2
        return carry

    lax.fori_loop(0, bx, first_pass, 0)

    for c in turn_x + arm_x:
        c.wait_recv()

    def prepare_x(t, carry):
        k, y = t // by, lax.rem(t, by)
        side = k // 2
        c = jnp.where(k < 2, k + bx - 2, k - 2) * by + y
        a = rim(k, bx, 0, bx)
        prepare(a + 2, 4 + y, px[side], c, A0[a, y, 2:3])
        return carry

    lax.fori_loop(0, 4 * by, prepare_x, 0, unroll=4)

    def second_pass_cell(x, y, lo):
        g0, g1, g2, k1, k2, k3, kk = (C[x, y, k:k + 1] for k in range(7))
        c = x * by + y
        for i in range(nocc):
            n = n_at(x, y, i)
            s1 = difference(lambda t: n_at(x, y + t, i))
            al = AL[x, y, i] + g1 * s1
            sc = k1 * n + k2 * al
            fl0 = sc * g0 + k3 * S0[x, y, i]
            fl1 = sc * g1 + k3 * s1
            fl2 = sc * g2 + k3 * S2[x, y, i]
            b = (kk * n + k1 * al) - difference(lambda t: pltpu.roll(fl2, (-t) % lanes, 1))
            S1[x, y, i] = s1
            f0[x + 2, y, i] = fl0
            f1[x, y + 2, i] = fl1
            base[x, y, i] = b
            deep = (2 * i) // nocc
            j = i % (nocc // 2)
            E2[j] = jnp.where(slot == c + cells * deep, pltpu.roll(fl2, 4 * c + half * deep, 1), E2[j])
            for k, v in enumerate((s1, b, fl0, fl1)):
                LO[lo, k, i] = rest(v)

    def wide(parts):
        return jnp.concatenate([p.reshape(pairs, lanes) for p in parts], axis=1)

    def gather(x, ys, at, start):
        (l0, l1), (y0, y1) = at, ys

        def pair(high, low):
            return wide(high), wide(low)

        def orbit(lo, y):
            left = pair([N[x + 4, y + 2], S0[x, y]], [NL[x, y], S0L[x, y]])
            return left, pair([base[x, y], f0[x + 2, y]], [LO[lo, 1], LO[lo, 2]])

        def products(left, right):
            return dot(left[0], right[0]), dot(left[1], right[0]), dot(left[0], right[1])

        p, q = products(*orbit(l0, y0)), products(*orbit(l1, y1))
        r = products(
            pair([S1[x, y0], S1[x, y1]], [LO[l0, 0], LO[l1, 0]]),
            pair([f1[x, y0 + 2], f1[x, y1 + 2]], [LO[l0, 3], LO[l1, 3]]),
        )
        one, two = sum(p[1:], p[0]), sum(q[1:], q[0])
        one, two = (one + r[0], two + (r[1] + r[2])) if x % 2 else (one + (r[1] + r[2]), two + r[0])
        for k, total in enumerate((one, two)):
            acc[k] = total if start else acc[k] + total

    def second_pass(ys, start, late):
        for x in range(bx):
            at = [2 * (x % 2), 2 * (x % 2) + 1]
            if late is not None:
                gather(*late)
            for lo, y in zip(at, ys):
                second_pass_cell(x, y, lo)
            late = (x, ys, at, start and x == 0)
        return late

    def across(depth):
        y = (4 - depth, by + 3 + depth)
        return lambda t: (4 + t // 2, jnp.where(lax.rem(t, 2) == 0, y[0], y[1]))

    for c in near_y[0]:
        c.wait_recv()
    multiply(2 * bx, across(1))
    late = second_pass((1, 2), True, None)
    for c in near_y[1]:
        c.wait_recv()
    corner = [
        put(
            W.at[near_src(bx, sx), near_dst(by, sy)],
            W.at[near_dst(bx, sx), near_dst(by, sy)],
            beside("gx", sx),
        )
        for sy in both
        for sx in both
    ]
    multiply(2 * bx, across(2))
    late = second_pass((0, 3), False, late)
    gather(*late)
    ends = [E2[i % (nocc // 2)] for i in range(nocc)]
    ends = [e if 2 * i < nocc else pltpu.roll(e, half, 1) for i, e in enumerate(ends)]
    right = jnp.concatenate(ends, axis=0)
    left, left_lo = LE[...].reshape(pairs, lanes), LEL[...].reshape(pairs, lanes)
    total = (acc[0] + acc[1]) + (dot(left, right) + dot(left_lo, right) + dot(left, rest(right)))
    for tx in range(nx):
        for ty in range(ny):
            for tz in range(nz):
                r = ((tx * ny + ty) * nz + tz) * rows_out
                part[tx, ty, tz] = total[r:r + rows_out]
    first = []
    for d in range(1, n_plane):
        tx, tz, target = plane(d)
        c = pltpu.make_async_remote_copy(
            src_ref=part.at[tx, :, tz], dst_ref=got.at[d],
            send_sem=send1.at[d], recv_sem=recv1.at[d],
            device_id=target, device_id_type=MESH,
        )
        c.start()
        first.append(c)
    z_out = [put(E2, ez.at[s], beside("gz", s)) for s in zsides]

    for c in far_x + corner:
        c.wait_recv()
    multiply(4 * by, lambda t: (rim(t // by, bx, 0, bx + 4), 4 + lax.rem(t, by)))
    multiply(16, lambda t: (rim(t // 4, bx, 2, bx + 2), rim(lax.rem(t, 4), by, 2, by + 2)))

    def at_x(t, carry):
        a, y = rim(t // by, bx, 0, bx), lax.rem(t, by)
        x = a - 2
        shifted = [vS[k, a, y + 2] for k in range(4)]
        c0, c1, c3 = A0[a, y, 0:1], A0[a, y, 1:2], A0[a, y, 3:4]
        for i in range(nocc):
            s0 = difference(lambda t: n_at(x + t, y, i))
            s1 = difference(lambda t: n_at(x, y + t, i))
            f0[a, y, i] = (c0 * s0 + c1 * s1) + (slope_z(x, y, i, shifted) + c3 * n_at(x, y, i))
        return carry

    lax.fori_loop(0, 4 * by, at_x, 0)

    for c in turn_y + arm_y:
        c.wait_recv()

    def prepare_y(t, carry):
        x, k = t // 4, lax.rem(t, 4)
        side = k // 2
        c = x * by + jnp.where(k < 2, k + by - 2, k - 2)
        b = rim(k, by, 0, by)
        prepare(4 + x, b + 2, py[side], c, A1[x, b, 2:3])
        return carry

    lax.fori_loop(0, 4 * bx, prepare_y, 0, unroll=4)

    def at_y(x, carry):
        for y in (-2, -1, by, by + 1):
            b = y + 2
            shifted = [vS[k, x + 2, b] for k in range(4)]
            c0, c1, c3 = A1[x, b, 0:1], A1[x, b, 1:2], A1[x, b, 3:4]
            for i in range(nocc):
                s0 = difference(lambda t: n_at(x + t, y, i))
                n = lambda t: n_at(x, y + t, i)
                if y == -2:
                    s1 = 8.0 * n(1) - n(2)
                elif y == -1:
                    s1 = 8.0 * (n(1) - n(-1)) - n(2)
                elif y == by:
                    s1 = 8.0 * (n(1) - n(-1)) + n(-2)
                else:
                    s1 = n(-2) - 8.0 * n(-1)
                f1[x, b, i] = (c0 * s0 + c1 * s1) + (slope_z(x, y, i, shifted) + c3 * n(0))
        return carry

    lax.fori_loop(0, bx, at_y, 0)

    for c in first:
        c.wait_recv()
    mine = part[gx, :, gz]
    for d in range(1, n_plane):
        mine = mine + got[d]
    acc2[...] = mine
    second = []
    for d in range(1, ny):
        t, target = column(d)
        c = pltpu.make_async_remote_copy(
            src_ref=acc2.at[t], dst_ref=got2.at[d],
            send_sem=send2.at[d], recv_sem=recv2.at[d],
            device_id=target, device_id_type=MESH,
        )
        c.start()
        second.append(c)

    for c in z_out:
        c.wait_recv()
    for j in range(nocc // 2):
        outer = ez[0, j] if nz == 2 else jnp.where((lane & 3) < 2, ez[1, j], ez[0, j])
        corr[j] = edge_terms(outer - E2[j], lane)
    for c in far_y:
        c.wait_recv()

    def assemble(x, carry):
        def far(y):
            return W[x + 4, y + 4, nocc:nocc + nvir]

        def slope_of(y):
            return A1[x, y + 2, 1:2]

        low1 = slope_of(-1) * far(-3)
        low2 = (slope_of(-2) * far(-4), -8.0 * slope_of(-2) * far(-3))
        top1 = -1.0 * slope_of(by) * far(by + 2)
        top2 = (8.0 * slope_of(by + 1) * far(by + 2), -1.0 * slope_of(by + 1) * far(by + 3))
        for i in range(nocc):
            o = [W[x + 4, y + 4, i:i + 1] for y in (-4, -3, by + 2, by + 3)]
            a = [f1[x, b, i] for b in range(by + 4)]
            a[0] = a[0] + (o[0] * low2[0] + o[1] * low2[1])
            a[1] = a[1] + o[1] * low1
            a[by + 2] = a[by + 2] + o[2] * top1
            a[by + 3] = a[by + 3] + (o[2] * top2[0] + o[3] * top2[1])
            deep = (2 * i) // nocc
            e = corr[i % (nocc // 2)]
            for y in range(by):
                c = x * by + y
                b = [f0[x + k, y, i] for k in (0, 1, 3, 4)]
                inner = (b[2] - b[1]) + (a[y + 3] - a[y + 1])
                outer = (b[3] - b[0]) + (a[y + 4] - a[y])
                turned = pltpu.roll(e, lax.rem(2 * lanes - 4 * c - half * deep, lanes), 1)
                v = base[x, y, i] - (8.0 * inner - outer)
                v = v - jnp.where(at_edge, turned, 0.0)
                pot[pl.ds(i * nvir * cells + c, nvir, stride=cells), :] = v
        return carry

    lax.fori_loop(0, bx, assemble, 0)
    for c in copies + first + second:
        c.wait_send()
    mine = acc2[gy]
    for d, c in enumerate(second):
        c.wait_recv()
        mine = mine + got2[d + 1]
    cas[...] = mine * (1.0 / (cells * lanes * nx * ny * nz))


def write_kernel(pot_in, cas_in, pot, cas, sem):
    rows = pot_in.shape[0] // sem.shape[0]
    out = []
    for k in range(sem.shape[0]):
        block = pl.ds(k * rows, rows)
        c = pltpu.make_async_copy(pot_in.at[block], pot.at[block], sem.at[k])
        c.start()
        out.append(c)
    cas[...] = cas_in[...]
    for c in out:
        c.wait()


def on_device(occupied, virtual, kernel_fields, density_grad):
    nocc, bx, by, lanes = occupied.shape
    nvir = virtual.shape[0]
    nx, ny, nz = (lax.axis_size(a) for a in ("gx", "gy", "gz"))
    devices = nx * ny * nz
    cells = bx * by
    pairs = nocc * nvir
    norb = nocc + nvir
    rows = pairs // devices
    sds = lambda *s: jax.ShapeDtypeStruct(s, F32)
    v32 = lambda *s: pltpu.VMEM(s, F32)
    dma = lambda n: pltpu.SemaphoreType.DMA((n,))
    vmem = pl.BlockSpec(memory_space=pltpu.VMEM)
    hbm = pl.BlockSpec(memory_space=pltpu.HBM)
    zs = 1 if nz == 2 else 2
    flat = lambda a: a.reshape(-1, lanes)
    outs = pl.pallas_call(
        flow_kernel,
        out_shape=(v32(pairs * cells, lanes), v32(rows, pairs)),
        in_specs=[hbm] * 4,
        out_specs=[vmem] * 2,
        scratch_shapes=[
            v32(nocc * cells, lanes), v32(nvir * cells, lanes), v32(4 * cells, lanes), v32(3 * cells, lanes),
            v32(bx + 8, by + 8, norb, lanes),
            v32(bx + 8, by + 4, nocc, nvir, lanes),
            v32(4, bx + 4, by + 4, nocc, lanes),
            v32(4, bx + 4, by + 4, nvir, lanes),
        ]
        + [v32(bx, by, nocc, nvir, lanes)] * 6
        + [
            v32(4, 4, nocc, nvir, lanes),
            v32(bx + 4, by, nocc, nvir, lanes),
            v32(bx, by + 4, nocc, nvir, lanes),
            v32(bx, by, nocc, nvir, lanes),
            v32(bx, by, 8, lanes), v32(bx + 4, by, 4, lanes), v32(bx, by + 4, 4, lanes),
            v32(nocc, lanes), v32(zs, nocc, lanes), v32(nocc, lanes), v32(2, nocc, lanes), v32(2, nocc, lanes),
            v32(nocc // 2, nvir, lanes), v32(zs, nocc // 2, nvir, lanes), v32(nocc // 2, nvir, lanes),
            v32(nocc, nvir, lanes), v32(nocc, nvir, lanes),
            v32(2, pairs, pairs),
            v32(nx, ny, nz, rows, pairs),
            v32(nx * nz, ny, rows, pairs),
            v32(ny, rows, pairs), v32(ny, rows, pairs),
            dma(28), dma(28), dma(4), dma(nx * nz), dma(nx * nz), dma(ny), dma(ny),
        ],
        compiler_params=pltpu.CompilerParams(
            collective_id=0, has_side_effects=True, vmem_limit_bytes=54 * MIB
        ),
        name="flow",
    )(*(pltpu.with_memory_space_constraint(flat(a), pltpu.HBM) for a in (occupied, virtual, kernel_fields, density_grad)))
    pot, casida = pl.pallas_call(
        write_kernel,
        out_shape=(sds(pairs * cells, lanes), sds(rows, pairs)),
        in_specs=[vmem] * 2,
        out_specs=(hbm, vmem),
        scratch_shapes=[dma(8)],
        compiler_params=pltpu.CompilerParams(vmem_limit_bytes=4 * MIB),
        name="write",
    )(*outs)
    return pot.reshape(pairs, bx, by, lanes), casida


def solution(mesh):
    spec = P(None, "gx", "gy", "gz")
    return jax.shard_map(
        on_device,
        mesh=mesh,
        in_specs=(spec,) * 4,
        out_specs=(spec, P(("gx", "gy", "gz"), None)),
        check_vma=False,
    )
```

time: 35.1 us -> 32 us (0.912)
  Pallas kernels: 34.3 us -> 31.2 us
    pallas_call x2, Pallas kernels: 34.3 us -> 31.2 us  [the longest x1 29.2 us: on_device(): pl.pallas_call(flow_kernel, out_shape=(v32(pairs * cells, lanes), v32(row...]
where the time goes in v3:
time: 32 us; the launch traced here: 31.8 us
  Pallas kernels  31.2 us (98%)
  between operations  0.64 us (2%)
    pallas_call x1, Pallas kernels, on_device(): pl.pallas_call(flow_kernel, out_shape=(v32(pairs * cells, lanes), v32(row...  29.2 us
    pallas_call x1, Pallas kernels, on_device(): pl.pallas_call(write_kernel, out_shape=(sds(pairs * cells, lanes), sds(ro...  1.97 us

profile of v3, /device:TPU:0, one launch (start us, length us, event | category | flops | bytes accessed | tf_op | source)
XLA Modules:
  0.0 31.8 jit_solution(15047575604652835876)
XLA Ops:
  0.6 29.2 %flow.1 = (f32[4096,128]{1,0:T(8,128)S(1)}, f32[8,256]{1,0:T(8,128)S(1)}) custom-call(f32[256,128]{1,0:T(8,128)} %bitcast.5, f32[256,128]{1,0:T(8,128)} %bitcast.6, f32[64,128]{1,0:T(8,128)} %bitcast.7, f32[48,128]{1,0:T(8,128)} %bitcast.8), custom_call_target="tpu_custom_call" | custom-call | tf_op jit(solution)/shard_map/flow/pallas_call | solution.py:527
  29.9 2.0 %write.1 = (f32[4096,128]{1,0:T(8,128)}, f32[8,256]{1,0:T(8,128)}) custom-call(f32[4096,128]{1,0:T(8,128)S(1)} %get-tuple-element.6.pot_in, f32[8,256]{1,0:T(8,128)S(1)} %get-tuple-element.7.cas_in), custom_call_target="tpu_custom_call" | custom-call | tf_op jit(solution)/shard_map/write/pallas_call | solution.py:560

commit v4 on v3

--- a/solution.py
+++ b/solution.py
@@ -45,7 +45,7 @@
     occ, vir, ker, grd, W, N, oS, vS, S0, S1, S2, AL, NL, S0L, LO, f0, f1, base, C, A0, A1,
     pk, wz, pkn, px, py, E2, ez, corr, LE, LEL,
     acc, part, got, acc2, got2,
-    send, recv, own, send1, recv1, send2, recv2,
+    send, recv, sendy, recvy, own, send1, recv1, send2, recv2,
 ):
     nx, ny, nz = (lax.axis_size(a) for a in ("gx", "gy", "gz"))
     gx, gy, gz = (lax.axis_index(a) for a in ("gx", "gy", "gz"))
@@ -71,7 +71,8 @@
     def beside(axis, side):
         v, n = {"gx": (gx, nx), "gy": (gy, ny), "gz": (gz, nz)}[axis]
         where = {"gx": gx, "gy": gy, "gz": gz}
-        where[axis] = lax.rem(v + 1, n) if side == 0 else lax.rem(v + n - 1, n)
+        step = (1, n - 1)[side] if isinstance(side, int) else jnp.where(side == 0, 1, n - 1)
+        where[axis] = lax.rem(v + step, n)
         return where
 
     taken = [
@@ -125,11 +126,11 @@
     def near_dst(b, side):
         return pl.ds(2, 2) if side == 0 else pl.ds(b + 4, 2)
 
-    def layer_src(b, side, depth):
-        return pl.ds(b + 4 - depth, 1) if side == 0 else pl.ds(3 + depth, 1)
-
-    def layer_dst(b, side, depth):
-        return pl.ds(4 - depth, 1) if side == 0 else pl.ds(b + 3 + depth, 1)
+    def layer_src(side, depth):
+        return pl.ds(jnp.where(side == 0, by + 4 - depth, 3 + depth), 1)
+
+    def layer_dst(side, depth):
+        return pl.ds(jnp.where(side == 0, 4 - depth, by + 3 + depth), 1)
 
     def far_src(b, side):
         return pl.ds(b, 2) if side == 0 else pl.ds(6, 2)
@@ -145,17 +146,19 @@
 
     zsides = range(1 if nz == 2 else 2)
     both = range(2)
-    near_y = [
-        [
-            put(
-                W.at[in_x, layer_src(by, s, depth)],
-                W.at[in_x, layer_dst(by, s, depth)],
-                beside("gy", s),
-            )
-            for s in both
-        ]
-        for depth in (1, 2)
-    ]
+    def layer_copy(s, depth):
+        k = 2 * (depth - 1) + s
+        return pltpu.make_async_remote_copy(
+            src_ref=W.at[in_x, layer_src(s, depth)], dst_ref=W.at[in_x, layer_dst(s, depth)],
+            send_sem=sendy.at[k], recv_sem=recvy.at[k],
+            device_id=beside("gy", s), device_id_type=MESH,
+        )
+
+    far_round = jnp.where(gy == ny - 1, 0, 1)
+    for depth in (1, 2):
+        layer_copy(far_round, depth).start()
+        layer_copy(1 - far_round, depth).start()
+    near_y = [[layer_copy(s, depth) for s in both] for depth in (1, 2)]
     near_x = [
         put(W.at[near_src(bx, s), in_y], W.at[near_dst(bx, s), in_y], beside("gx", s)) for s in both
     ]
@@ -310,18 +313,24 @@
             left = pair([N[x + 4, y + 2], S0[x, y]], [NL[x, y], S0L[x, y]])
             return left, pair([base[x, y], f0[x + 2, y]], [LO[lo, 1], LO[lo, 2]])
 
-        def products(left, right):
-            return dot(left[0], right[0]), dot(left[1], right[0]), dot(left[0], right[1])
-
-        p, q = products(*orbit(l0, y0)), products(*orbit(l1, y1))
-        r = products(
+        first, second = orbit(l0, y0), orbit(l1, y1)
+        third = (
             pair([S1[x, y0], S1[x, y1]], [LO[l0, 0], LO[l1, 0]]),
             pair([f1[x, y0 + 2], f1[x, y1 + 2]], [LO[l0, 3], LO[l1, 3]]),
         )
-        one, two = sum(p[1:], p[0]), sum(q[1:], q[0])
-        one, two = (one + r[0], two + (r[1] + r[2])) if x % 2 else (one + (r[1] + r[2]), two + r[0])
-        for k, total in enumerate((one, two)):
-            acc[k] = total if start else acc[k] + total
+
+        def beside_(parts):
+            return jnp.concatenate(parts, axis=1)
+
+        left = [beside_([first[0][k], second[0][k]]) for k in range(2)]
+        right = [beside_([first[1][k], second[1][k]]) for k in range(2)]
+        top = dot(jnp.concatenate(left, axis=0), right[0])
+        low_part = dot(
+            beside_([left[0], third[0][0], third[0][0], third[0][1]]),
+            beside_([right[1], third[1][0], third[1][1], third[1][0]]),
+        )
+        total = (top[0:pairs] + top[pairs:]) + low_part
+        acc[...] = total if start else acc[...] + total
 
     def second_pass(ys, start, late):
         for x in range(bx):
@@ -337,21 +346,25 @@
         y = (4 - depth, by + 3 + depth)
         return lambda t: (4 + t // 2, jnp.where(lax.rem(t, 2) == 0, y[0], y[1]))
 
+    def turn_corner(depth):
+        return [
+            put(
+                W.at[near_src(bx, sx), layer_dst(sy, depth)],
+                W.at[near_dst(bx, sx), layer_dst(sy, depth)],
+                beside("gx", sx),
+            )
+            for sy in both
+            for sx in both
+        ]
+
     for c in near_y[0]:
         c.wait_recv()
+    corner = turn_corner(1)
     multiply(2 * bx, across(1))
     late = second_pass((1, 2), True, None)
     for c in near_y[1]:
         c.wait_recv()
-    corner = [
-        put(
-            W.at[near_src(bx, sx), near_dst(by, sy)],
-            W.at[near_dst(bx, sx), near_dst(by, sy)],
-            beside("gx", sx),
-        )
-        for sy in both
-        for sx in both
-    ]
+    corner += turn_corner(2)
     multiply(2 * bx, across(2))
     late = second_pass((0, 3), False, late)
     gather(*late)
@@ -359,14 +372,14 @@
     ends = [e if 2 * i < nocc else pltpu.roll(e, half, 1) for i, e in enumerate(ends)]
     right = jnp.concatenate(ends, axis=0)
     left, left_lo = LE[...].reshape(pairs, lanes), LEL[...].reshape(pairs, lanes)
-    total = (acc[0] + acc[1]) + (dot(left, right) + dot(left_lo, right) + dot(left, rest(right)))
+    total = acc[...] + (dot(left, right) + dot(left_lo, right) + dot(left, rest(right)))
     for tx in range(nx):
         for ty in range(ny):
             for tz in range(nz):
                 r = ((tx * ny + ty) * nz + tz) * rows_out
                 part[tx, ty, tz] = total[r:r + rows_out]
     first = []
-    for d in range(1, n_plane):
+    for d in sorted(range(1, n_plane), key=lambda d: abs(2 * d - n_plane)):
         tx, tz, target = plane(d)
         c = pltpu.make_async_remote_copy(
             src_ref=part.at[tx, :, tz], dst_ref=got.at[d],
@@ -486,7 +499,7 @@
         return carry
 
     lax.fori_loop(0, bx, assemble, 0)
-    for c in copies + first + second:
+    for c in copies + near_y[0] + near_y[1] + first + second:
         c.wait_send()
     mine = acc2[gy]
     for d, c in enumerate(second):
@@ -546,11 +559,11 @@
             v32(nocc, lanes), v32(zs, nocc, lanes), v32(nocc, lanes), v32(2, nocc, lanes), v32(2, nocc, lanes),
             v32(nocc // 2, nvir, lanes), v32(zs, nocc // 2, nvir, lanes), v32(nocc // 2, nvir, lanes),
             v32(nocc, nvir, lanes), v32(nocc, nvir, lanes),
-            v32(2, pairs, pairs),
+            v32(pairs, pairs),
             v32(nx, ny, nz, rows, pairs),
             v32(nx * nz, ny, rows, pairs),
             v32(ny, rows, pairs), v32(ny, rows, pairs),
-            dma(28), dma(28), dma(4), dma(nx * nz), dma(nx * nz), dma(ny), dma(ny),
+            dma(28), dma(28), dma(4), dma(4), dma(4), dma(nx * nz), dma(nx * nz), dma(ny), dma(ny),
         ],
         compiler_params=pltpu.CompilerParams(
             collective_id=0, has_side_effects=True, vmem_limit_bytes=54 * MIB

time: 32 us -> 30.2 us (0.944)
  Pallas kernels: 31.2 us -> 29.4 us
    pallas_call x1, Pallas kernels: 29.2 us -> 27.4 us  [on_device(): pl.pallas_call(flow_kernel, out_shape=(v32(pairs * cells, lanes), v32(row...]
where the time goes in v4:
time: 30.2 us; the launch traced here: 30 us
  Pallas kernels  29.4 us (97%)
  between operations  0.64 us (2%)
    pallas_call x1, Pallas kernels, on_device(): pl.pallas_call(flow_kernel, out_shape=(v32(pairs * cells, lanes), v32(row...  27.4 us
    pallas_call x1, Pallas kernels, on_device(): pl.pallas_call(write_kernel, out_shape=(sds(pairs * cells, lanes), sds(ro...  1.97 us

profile of v4, /device:TPU:0, one launch (start us, length us, event | category | flops | bytes accessed | tf_op | source)
XLA Modules:
  0.0 30.0 jit_solution(5176665036990429970)
XLA Ops:
  0.6 27.4 %flow.1 = (f32[4096,128]{1,0:T(8,128)S(1)}, f32[8,256]{1,0:T(8,128)S(1)}) custom-call(f32[256,128]{1,0:T(8,128)} %bitcast.5, f32[256,128]{1,0:T(8,128)} %bitcast.6, f32[64,128]{1,0:T(8,128)} %bitcast.7, f32[48,128]{1,0:T(8,128)} %bitcast.8), custom_call_target="tpu_custom_call" | custom-call | tf_op jit(solution)/shard_map/flow/pallas_call | solution.py:540
  28.1 2.0 %write.1 = (f32[4096,128]{1,0:T(8,128)}, f32[8,256]{1,0:T(8,128)}) custom-call(f32[4096,128]{1,0:T(8,128)S(1)} %get-tuple-element.6.pot_in, f32[8,256]{1,0:T(8,128)S(1)} %get-tuple-element.7.cas_in), custom_call_target="tpu_custom_call" | custom-call | tf_op jit(solution)/shard_map/write/pallas_call | solution.py:573

commit v5 on v4

--- a/solution.py
+++ b/solution.py
@@ -238,10 +238,6 @@
         LE[i] = e
         LEL[i] = rest(e)
 
-    for c in near_x:
-        c.wait_recv()
-    multiply(4 * by, lambda t: (rim(t // by, bx, 2, bx + 2), 4 + lax.rem(t, by)))
-
     def slope_z(x, y, i, shifted):
         p = [oS[k, x + 2, y + 2, i:i + 1] * shifted[k] for k in range(4)]
         return (p[0] - p[1]) - (p[2] - p[3])
@@ -249,34 +245,31 @@
     def n_at(x, y, i):
         return N[x + 4, y + 2, i]
 
-    def first_pass(x, carry):
+    def own_pass(x, carry):
         for y in range(by):
-            g0, g2 = C[x, y, 0:1], C[x, y, 2:3]
             shifted = [vS[k, x + 2, y + 2] for k in range(4)]
             for i in range(nocc):
                 NL[x, y, i] = rest(n_at(x, y, i))
-                s2 = slope_z(x, y, i, shifted)
-                S2[x, y, i] = s2
+                S2[x, y, i] = slope_z(x, y, i, shifted)
+        return carry
+
+    lax.fori_loop(0, bx, own_pass, 0)
+
+    for c in near_x:
+        c.wait_recv()
+    multiply(4 * by, lambda t: (rim(t // by, bx, 2, bx + 2), 4 + lax.rem(t, by)))
+
+    def x_pass(x, carry):
+        for y in range(by):
+            g0, g2 = C[x, y, 0:1], C[x, y, 2:3]
+            for i in range(nocc):
                 s0 = difference(lambda t: n_at(x + t, y, i))
                 S0[x, y, i] = s0
                 S0L[x, y, i] = rest(s0)
-                AL[x, y, i] = g0 * s0 + g2 * s2
-        return carry
-
-    lax.fori_loop(0, bx, first_pass, 0)
-
-    for c in turn_x + arm_x:
-        c.wait_recv()
-
-    def prepare_x(t, carry):
-        k, y = t // by, lax.rem(t, by)
-        side = k // 2
-        c = jnp.where(k < 2, k + bx - 2, k - 2) * by + y
-        a = rim(k, bx, 0, bx)
-        prepare(a + 2, 4 + y, px[side], c, A0[a, y, 2:3])
-        return carry
-
-    lax.fori_loop(0, 4 * by, prepare_x, 0, unroll=4)
+                AL[x, y, i] = g0 * s0 + g2 * S2[x, y, i]
+        return carry
+
+    lax.fori_loop(0, bx, x_pass, 0)
 
     def second_pass_cell(x, y, lo):
         g0, g1, g2, k1, k2, k3, kk = (C[x, y, k:k + 1] for k in range(7))
@@ -390,6 +383,19 @@
         first.append(c)
     z_out = [put(E2, ez.at[s], beside("gz", s)) for s in zsides]
 
+    for c in turn_x + arm_x:
+        c.wait_recv()
+
+    def prepare_x(t, carry):
+        k, y = t // by, lax.rem(t, by)
+        side = k // 2
+        c = jnp.where(k < 2, k + bx - 2, k - 2) * by + y
+        a = rim(k, bx, 0, bx)
+        prepare(a + 2, 4 + y, px[side], c, A0[a, y, 2:3])
+        return carry
+
+    lax.fori_loop(0, 4 * by, prepare_x, 0, unroll=4)
+
     for c in far_x + corner:
         c.wait_recv()
     multiply(4 * by, lambda t: (rim(t // by, bx, 0, bx + 4), 4 + lax.rem(t, by)))
@@ -509,14 +515,14 @@
 
 
 def write_kernel(pot_in, cas_in, pot, cas, sem):
-    rows = pot_in.shape[0] // sem.shape[0]
-    out = []
-    for k in range(sem.shape[0]):
+    parts = sem.shape[0] - 1
+    rows = pot_in.shape[0] // parts
+    out = [pltpu.make_async_copy(cas_in, cas, sem.at[parts])]
+    for k in range(parts):
         block = pl.ds(k * rows, rows)
-        c = pltpu.make_async_copy(pot_in.at[block], pot.at[block], sem.at[k])
+        out.append(pltpu.make_async_copy(pot_in.at[block], pot.at[block], sem.at[k]))
+    for c in out:
         c.start()
-        out.append(c)
-    cas[...] = cas_in[...]
     for c in out:
         c.wait()
 
@@ -574,8 +580,8 @@
         write_kernel,
         out_shape=(sds(pairs * cells, lanes), sds(rows, pairs)),
         in_specs=[vmem] * 2,
-        out_specs=(hbm, vmem),
-        scratch_shapes=[dma(8)],
+        out_specs=(hbm, hbm),
+        scratch_shapes=[dma(9)],
         compiler_params=pltpu.CompilerParams(vmem_limit_bytes=4 * MIB),
         name="write",
     )(*outs)

time: 30.2 us -> 28.5 us (0.944)
  Pallas kernels: 29.4 us -> 27.7 us
    pallas_call x1, Pallas kernels: 27.4 us -> 26.3 us  [on_device(): pl.pallas_call(flow_kernel, out_shape=(v32(pairs * cells, lanes), v32(row...]
    pallas_call x1, Pallas kernels: 1.97 us -> 1.39 us  [on_device(): pl.pallas_call(write_kernel, out_shape=(sds(pairs * cells, lanes), sds(ro...]
where the time goes in v5:
time: 28.5 us; the launch traced here: 28.4 us
  Pallas kernels  27.7 us (97%)
  between operations  0.64 us (2%)
    pallas_call x1, Pallas kernels, on_device(): pl.pallas_call(flow_kernel, out_shape=(v32(pairs * cells, lanes), v32(row...  26.3 us
    pallas_call x1, Pallas kernels, on_device(): pl.pallas_call(write_kernel, out_shape=(sds(pairs * cells, lanes), sds(ro...  1.39 us

profile of v5, /device:TPU:0, one launch (start us, length us, event | category | flops | bytes accessed | tf_op | source)
XLA Modules:
  0.0 28.4 jit_solution(13867632717697422436)
XLA Ops:
  0.6 26.3 %flow.1 = (f32[4096,128]{1,0:T(8,128)S(1)}, f32[8,256]{1,0:T(8,128)S(1)}) custom-call(f32[256,128]{1,0:T(8,128)} %bitcast.5, f32[256,128]{1,0:T(8,128)} %bitcast.6, f32[64,128]{1,0:T(8,128)} %bitcast.7, f32[48,128]{1,0:T(8,128)} %bitcast.8), custom_call_target="tpu_custom_call" | custom-call | tf_op jit(solution)/shard_map/flow/pallas_call | solution.py:546
  27.0 1.4 %write.1 = (f32[4096,128]{1,0:T(8,128)}, f32[8,256]{1,0:T(8,128)}) custom-call(f32[4096,128]{1,0:T(8,128)S(1)} %get-tuple-element.6.pot_in, f32[8,256]{1,0:T(8,128)S(1)} %get-tuple-element.7.cas_in), custom_call_target="tpu_custom_call" | custom-call | tf_op jit(solution)/shard_map/write/pallas_call | solution.py:579

commit v6 on v5

--- a/solution.py
+++ b/solution.py
@@ -104,8 +104,6 @@
         x, y, o, v = own_rows(c)
         W[x + 4, y + 4, 0:nocc] = o
         W[x + 4, y + 4, nocc:nocc + nvir] = v
-    pl.semaphore_wait(barrier, n_plane - 1 + ny - 1)
-
     copies = []
 
     def put(src, dst, device):
@@ -118,50 +116,6 @@
         copies.append(c)
         return c
 
-    in_x, in_y = pl.ds(4, bx), pl.ds(4, by)
-
-    def near_src(b, side):
-        return pl.ds(b + 2, 2) if side == 0 else pl.ds(4, 2)
-
-    def near_dst(b, side):
-        return pl.ds(2, 2) if side == 0 else pl.ds(b + 4, 2)
-
-    def layer_src(side, depth):
-        return pl.ds(jnp.where(side == 0, by + 4 - depth, 3 + depth), 1)
-
-    def layer_dst(side, depth):
-        return pl.ds(jnp.where(side == 0, 4 - depth, by + 3 + depth), 1)
-
-    def far_src(b, side):
-        return pl.ds(b, 2) if side == 0 else pl.ds(6, 2)
-
-    def far_dst(b, side):
-        return pl.ds(0, 2) if side == 0 else pl.ds(b + 6, 2)
-
-    def arm_src(b, side):
-        return pl.ds(b, 2) if side == 0 else pl.ds(2, 2)
-
-    def arm_dst(b, side):
-        return pl.ds(0, 2) if side == 0 else pl.ds(b + 2, 2)
-
-    zsides = range(1 if nz == 2 else 2)
-    both = range(2)
-    def layer_copy(s, depth):
-        k = 2 * (depth - 1) + s
-        return pltpu.make_async_remote_copy(
-            src_ref=W.at[in_x, layer_src(s, depth)], dst_ref=W.at[in_x, layer_dst(s, depth)],
-            send_sem=sendy.at[k], recv_sem=recvy.at[k],
-            device_id=beside("gy", s), device_id_type=MESH,
-        )
-
-    far_round = jnp.where(gy == ny - 1, 0, 1)
-    for depth in (1, 2):
-        layer_copy(far_round, depth).start()
-        layer_copy(1 - far_round, depth).start()
-    near_y = [[layer_copy(s, depth) for s in both] for depth in (1, 2)]
-    near_x = [
-        put(W.at[near_src(bx, s), in_y], W.at[near_dst(bx, s), in_y], beside("gx", s)) for s in both
-    ]
     taken[2].wait()
     taken[3].wait()
     packed = jnp.zeros((nocc, lanes), F32)
@@ -178,11 +132,6 @@
             a = [q * g[k] + k3 if k == m else q * g[k] for k in range(3)]
             ref[...] = jnp.concatenate(a + [k1 * g[m]], axis=0)
     pk[...] = packed
-    z_in = [put(pk, wz.at[s], beside("gz", s)) for s in zsides]
-    arm_x = [put(A0.at[arm_src(bx, s)], A0.at[arm_dst(bx, s)], beside("gx", s)) for s in both]
-    arm_y = [
-        put(A1.at[:, arm_src(by, s)], A1.at[:, arm_dst(by, s)], beside("gy", s)) for s in both
-    ]
 
     def multiply(count, place, unroll=2):
         def body(t, carry):
@@ -199,6 +148,73 @@
 
     multiply(cells, lambda t: (4 + t // by, 4 + lax.rem(t, by)))
 
+    pl.semaphore_wait(barrier, n_plane - 1 + ny - 1)
+    in_x, in_y = pl.ds(4, bx), pl.ds(4, by)
+
+    def near_src(b, side):
+        return pl.ds(b + 2, 2) if side == 0 else pl.ds(4, 2)
+
+    def near_dst(b, side):
+        return pl.ds(2, 2) if side == 0 else pl.ds(b + 4, 2)
+
+    def layer_src(side, depth):
+        return pl.ds(jnp.where(side == 0, by + 4 - depth, 3 + depth), 1)
+
+    def layer_dst(side, depth):
+        return pl.ds(jnp.where(side == 0, 4 - depth, by + 3 + depth), 1)
+
+    def far_src(b, side):
+        return pl.ds(b, 2) if side == 0 else pl.ds(6, 2)
+
+    def far_dst(b, side):
+        return pl.ds(0, 2) if side == 0 else pl.ds(b + 6, 2)
+
+    def arm_src(b, side):
+        return pl.ds(b, 2) if side == 0 else pl.ds(2, 2)
+
+    def arm_dst(b, side):
+        return pl.ds(0, 2) if side == 0 else pl.ds(b + 2, 2)
+
+    zsides = range(1 if nz == 2 else 2)
+    both = range(2)
+    def layer_copy(s, depth):
+        k = 2 * (depth - 1) + s
+        return pltpu.make_async_remote_copy(
+            src_ref=W.at[in_x, layer_src(s, depth)], dst_ref=W.at[in_x, layer_dst(s, depth)],
+            send_sem=sendy.at[k], recv_sem=recvy.at[k],
+            device_id=beside("gy", s), device_id_type=MESH,
+        )
+
+    far_round = jnp.where(gy == ny - 1, 0, 1)
+    for depth in (1, 2):
+        layer_copy(far_round, depth).start()
+        layer_copy(1 - far_round, depth).start()
+    near_y = [[layer_copy(s, depth) for s in both] for depth in (1, 2)]
+    z_in = [put(pk, wz.at[s], beside("gz", s)) for s in zsides]
+
+    def x_copy(s):
+        return pltpu.make_async_remote_copy(
+            src_ref=W.at[pl.ds(jnp.where(s == 0, bx + 2, 4), 2), in_y],
+            dst_ref=W.at[pl.ds(jnp.where(s == 0, 2, bx + 4), 2), in_y],
+            send_sem=sendy.at[4 + s], recv_sem=recvy.at[4 + s],
+            device_id=beside("gx", s), device_id_type=MESH,
+        )
+
+    near_x = [x_copy(s) for s in both]
+    for c in near_x:
+        c.start()
+    arm_x = [put(A0.at[arm_src(bx, s)], A0.at[arm_dst(bx, s)], beside("gx", s)) for s in both]
+    arm_y = [
+        put(A1.at[:, arm_src(by, s)], A1.at[:, arm_dst(by, s)], beside("gy", s)) for s in both
+    ]
+
+    def low_pass(x, carry):
+        for y in range(by):
+            for i in range(nocc):
+                NL[x, y, i] = rest(N[x + 4, y + 2, i])
+        return carry
+
+    lax.fori_loop(0, bx, low_pass, 0)
     for c in z_in:
         c.wait_recv()
     low = (lanes_of((nocc, lanes)) & 3) < 2
@@ -214,8 +230,8 @@
     ]
 
     def prepare(x, y, edges, c, fold):
-        ao = pltpu.roll(edges, lax.rem(lanes - 4 * c, lanes), 1)
-        av = pltpu.roll(edges, lax.rem(lanes + half - 4 * c, lanes), 1)
+        ao = pltpu.roll(edges, (lanes - 4 * c) % lanes, 1)
+        av = pltpu.roll(edges, (lanes + half - 4 * c) % lanes, 1)
         o_own, v_own = W[x, y, 0:nocc], W[x, y, nocc:nocc + nvir]
         for k, s in enumerate(SHIFTS):
             m = lane < s if s > 0 else lane >= lanes + s
@@ -224,11 +240,8 @@
             oS[k, x - 2, y - 2] = factor * pltpu.roll(jnp.where(m, ao, o_own), (-s) % lanes, 1)
             vS[k, x - 2, y - 2] = pltpu.roll(jnp.where(m, av, v_own), (-s) % lanes, 1)
 
-    def prepare_center(t, carry):
-        prepare(4 + t // by, 4 + lax.rem(t, by), pkn[...], t, None)
-        return carry
-
-    lax.fori_loop(0, cells, prepare_center, 0, unroll=4)
+    for t in range(cells):
+        prepare(4 + t // by, 4 + t % by, z_edges, t, None)
 
     own_o, own_v = pk[...], pltpu.roll(pk[...], half, 1)
     nb_o, nb_v = z_edges, pltpu.roll(z_edges, half, 1)
@@ -249,16 +262,13 @@
         for y in range(by):
             shifted = [vS[k, x + 2, y + 2] for k in range(4)]
             for i in range(nocc):
-                NL[x, y, i] = rest(n_at(x, y, i))
                 S2[x, y, i] = slope_z(x, y, i, shifted)
         return carry
 
     lax.fori_loop(0, bx, own_pass, 0)
 
-    for c in near_x:
-        c.wait_recv()
-    multiply(4 * by, lambda t: (rim(t // by, bx, 2, bx + 2), 4 + lax.rem(t, by)))
-
+    early = 1 - lax.rem(gx, 2)
+    x_done = [early, 1 - early]
     def x_pass(x, carry):
         for y in range(by):
             g0, g2 = C[x, y, 0:1], C[x, y, 2:3]
@@ -269,7 +279,12 @@
                 AL[x, y, i] = g0 * s0 + g2 * S2[x, y, i]
         return carry
 
-    lax.fori_loop(0, bx, x_pass, 0)
+    for s in x_done:
+        x_copy(s).wait_recv()
+        at = jnp.where(s == 0, 2, bx + 4)
+        multiply(2 * by, lambda t: (at + t // by, 4 + lax.rem(t, by)))
+        lo = jnp.where(s == 0, 0, bx - 2)
+        lax.fori_loop(0, 2, lambda t, carry: x_pass(lo + t, carry), 0)
 
     def second_pass_cell(x, y, lo):
         g0, g1, g2, k1, k2, k3, kk = (C[x, y, k:k + 1] for k in range(7))
@@ -386,15 +401,10 @@
     for c in turn_x + arm_x:
         c.wait_recv()
 
-    def prepare_x(t, carry):
-        k, y = t // by, lax.rem(t, by)
-        side = k // 2
-        c = jnp.where(k < 2, k + bx - 2, k - 2) * by + y
-        a = rim(k, bx, 0, bx)
-        prepare(a + 2, 4 + y, px[side], c, A0[a, y, 2:3])
-        return carry
-
-    lax.fori_loop(0, 4 * by, prepare_x, 0, unroll=4)
+    for a in (0, 1, bx + 2, bx + 3):
+        edges = px[0] if a < 2 else px[1]
+        for y in range(by):
+            prepare(a + 2, 4 + y, edges, (a - 2) % bx * by + y, A0[a, y, 2:3])
 
     for c in far_x + corner:
         c.wait_recv()
@@ -417,15 +427,10 @@
     for c in turn_y + arm_y:
         c.wait_recv()
 
-    def prepare_y(t, carry):
-        x, k = t // 4, lax.rem(t, 4)
-        side = k // 2
-        c = x * by + jnp.where(k < 2, k + by - 2, k - 2)
-        b = rim(k, by, 0, by)
-        prepare(4 + x, b + 2, py[side], c, A1[x, b, 2:3])
-        return carry
-
-    lax.fori_loop(0, 4 * bx, prepare_y, 0, unroll=4)
+    for b in (0, 1, by + 2, by + 3):
+        edges = py[0] if b < 2 else py[1]
+        for x in range(bx):
+            prepare(4 + x, b + 2, edges, x * by + (b - 2) % by, A1[x, b, 2:3])
 
     def at_y(x, carry):
         for y in (-2, -1, by, by + 1):
@@ -505,7 +510,7 @@
         return carry
 
     lax.fori_loop(0, bx, assemble, 0)
-    for c in copies + near_y[0] + near_y[1] + first + second:
+    for c in copies + near_y[0] + near_y[1] + near_x + first + second:
         c.wait_send()
     mine = acc2[gy]
     for d, c in enumerate(second):
@@ -569,7 +574,7 @@
             v32(nx, ny, nz, rows, pairs),
             v32(nx * nz, ny, rows, pairs),
             v32(ny, rows, pairs), v32(ny, rows, pairs),
-            dma(28), dma(28), dma(4), dma(4), dma(4), dma(nx * nz), dma(nx * nz), dma(ny), dma(ny),
+            dma(28), dma(28), dma(6), dma(6), dma(4), dma(nx * nz), dma(nx * nz), dma(ny), dma(ny),
         ],
         compiler_params=pltpu.CompilerParams(
             collective_id=0, has_side_effects=True, vmem_limit_bytes=54 * MIB

time: 28.5 us -> 28.9 us (1.014)
  Pallas kernels: 27.7 us -> 28.1 us
    pallas_call x1, Pallas kernels: 26.3 us -> 26.7 us  [on_device(): pl.pallas_call(flow_kernel, out_shape=(v32(pairs * cells, lanes), v32(row...]
where the time goes in v6:
time: 28.9 us; the launch traced here: 28.8 us
  Pallas kernels  28.1 us (97%)
  between operations  0.64 us (2%)
    pallas_call x1, Pallas kernels, on_device(): pl.pallas_call(flow_kernel, out_shape=(v32(pairs * cells, lanes), v32(row...  26.7 us
    pallas_call x1, Pallas kernels, on_device(): pl.pallas_call(write_kernel, out_shape=(sds(pairs * cells, lanes), sds(ro...  1.39 us

profile of v6, /device:TPU:0, one launch (start us, length us, event | category | flops | bytes accessed | tf_op | source)
XLA Modules:
  0.0 28.8 jit_solution(3245090502780165374)
XLA Ops:
  0.6 26.7 %flow.1 = (f32[4096,128]{1,0:T(8,128)S(1)}, f32[8,256]{1,0:T(8,128)S(1)}) custom-call(f32[256,128]{1,0:T(8,128)} %bitcast.5, f32[256,128]{1,0:T(8,128)} %bitcast.6, f32[64,128]{1,0:T(8,128)} %bitcast.7, f32[48,128]{1,0:T(8,128)} %bitcast.8), custom_call_target="tpu_custom_call" | custom-call | tf_op jit(solution)/shard_map/flow/pallas_call | solution.py:551
  27.4 1.4 %write.1 = (f32[4096,128]{1,0:T(8,128)}, f32[8,256]{1,0:T(8,128)}) custom-call(f32[4096,128]{1,0:T(8,128)S(1)} %get-tuple-element.6.pot_in, f32[8,256]{1,0:T(8,128)S(1)} %get-tuple-element.7.cas_in), custom_call_target="tpu_custom_call" | custom-call | tf_op jit(solution)/shard_map/write/pallas_call | solution.py:584

commit v7 on v5

--- a/solution.py
+++ b/solution.py
@@ -42,7 +42,7 @@
 def flow_kernel(
     occ_in, vir_in, ker_in, grd_in,
     pot, cas,
-    occ, vir, ker, grd, W, N, oS, vS, S0, S1, S2, AL, NL, S0L, LO, f0, f1, base, C, A0, A1,
+    occ, vir, ker, grd, W, N, oS, vS, S0, S1, S2, NL, S0L, LO, f0, f1, base, C, A0, A1,
     pk, wz, pkn, px, py, E2, ez, corr, LE, LEL,
     acc, part, got, acc2, got2,
     send, recv, sendy, recvy, own, send1, recv1, send2, recv2,
@@ -159,16 +159,29 @@
         layer_copy(far_round, depth).start()
         layer_copy(1 - far_round, depth).start()
     near_y = [[layer_copy(s, depth) for s in both] for depth in (1, 2)]
-    near_x = [
-        put(W.at[near_src(bx, s), in_y], W.at[near_dst(bx, s), in_y], beside("gx", s)) for s in both
-    ]
-    taken[2].wait()
-    taken[3].wait()
+
+    def x_copy(s):
+        return pltpu.make_async_remote_copy(
+            src_ref=W.at[pl.ds(jnp.where(s == 0, bx + 2, 4), 2), in_y],
+            dst_ref=W.at[pl.ds(jnp.where(s == 0, 2, bx + 4), 2), in_y],
+            send_sem=sendy.at[4 + s], recv_sem=recvy.at[4 + s],
+            device_id=beside("gx", s), device_id_type=MESH,
+        )
+
+    near_x = [x_copy(s) for s in both]
+    for c in near_x:
+        c.start()
     packed = jnp.zeros((nocc, lanes), F32)
     for c in range(cells):
         x, y, o, v = own_rows(c)
         packed += pltpu.roll(jnp.where(at_edge, o, 0.0), 4 * c, 1)
         packed += pltpu.roll(jnp.where(at_edge, v, 0.0), 4 * c + half, 1)
+    pk[...] = packed
+    z_in = [put(pk, wz.at[s], beside("gz", s)) for s in zsides]
+    taken[2].wait()
+    taken[3].wait()
+    for c in range(cells):
+        x, y = divmod(c, by)
         g = [grd[pl.ds(k * cells + c, 1), :] for k in range(3)]
         f = [ker[pl.ds(k * cells + c, 1), :] for k in range(4)]
         k1, k2, k3 = f[1] * (1.0 / 12.0), f[2] * (1.0 / 144.0), f[3] * (1.0 / 144.0)
@@ -177,8 +190,6 @@
             q = k2 * g[m]
             a = [q * g[k] + k3 if k == m else q * g[k] for k in range(3)]
             ref[...] = jnp.concatenate(a + [k1 * g[m]], axis=0)
-    pk[...] = packed
-    z_in = [put(pk, wz.at[s], beside("gz", s)) for s in zsides]
     arm_x = [put(A0.at[arm_src(bx, s)], A0.at[arm_dst(bx, s)], beside("gx", s)) for s in both]
     arm_y = [
         put(A1.at[:, arm_src(by, s)], A1.at[:, arm_dst(by, s)], beside("gy", s)) for s in both
@@ -255,34 +266,41 @@
 
     lax.fori_loop(0, bx, own_pass, 0)
 
-    for c in near_x:
-        c.wait_recv()
-    multiply(4 * by, lambda t: (rim(t // by, bx, 2, bx + 2), 4 + lax.rem(t, by)))
-
     def x_pass(x, carry):
         for y in range(by):
-            g0, g2 = C[x, y, 0:1], C[x, y, 2:3]
+            g0, g1, g2, k1, k2, k3, kk = (C[x, y, k:k + 1] for k in range(7))
             for i in range(nocc):
+                n = n_at(x, y, i)
                 s0 = difference(lambda t: n_at(x + t, y, i))
                 S0[x, y, i] = s0
                 S0L[x, y, i] = rest(s0)
-                AL[x, y, i] = g0 * s0 + g2 * S2[x, y, i]
-        return carry
-
-    lax.fori_loop(0, bx, x_pass, 0)
+                s2 = S2[x, y, i]
+                al = g0 * s0 + g2 * s2
+                sc = k1 * n + k2 * al
+                f0[x + 2, y, i] = sc * g0 + k3 * s0
+                f1[x, y + 2, i] = sc * g1
+                S2[x, y, i] = sc * g2 + k3 * s2
+                base[x, y, i] = kk * n + k1 * al
+        return carry
+
+    early = 1 - lax.rem(gx, 2)
+    for s in (early, 1 - early):
+        x_copy(s).wait_recv()
+        at = jnp.where(s == 0, 2, bx + 4)
+        multiply(2 * by, lambda t: (at + t // by, 4 + lax.rem(t, by)))
+        lo = jnp.where(s == 0, 0, bx - 2)
+        lax.fori_loop(0, 2, lambda t, carry: x_pass(lo + t, carry), 0)
 
     def second_pass_cell(x, y, lo):
-        g0, g1, g2, k1, k2, k3, kk = (C[x, y, k:k + 1] for k in range(7))
+        w0, w1, w2, wb = (A1[x, y + 2, k:k + 1] for k in range(4))
         c = x * by + y
         for i in range(nocc):
-            n = n_at(x, y, i)
             s1 = difference(lambda t: n_at(x, y + t, i))
-            al = AL[x, y, i] + g1 * s1
-            sc = k1 * n + k2 * al
-            fl0 = sc * g0 + k3 * S0[x, y, i]
-            fl1 = sc * g1 + k3 * s1
-            fl2 = sc * g2 + k3 * S2[x, y, i]
-            b = (kk * n + k1 * al) - difference(lambda t: pltpu.roll(fl2, (-t) % lanes, 1))
+            fl0 = f0[x + 2, y, i] + w0 * s1
+            fl1 = f1[x, y + 2, i] + w1 * s1
+            fl2 = S2[x, y, i] + w2 * s1
+            turned = difference(lambda t: pltpu.roll(fl2, (-t) % lanes, 1))
+            b = (base[x, y, i] + wb * s1) - turned
             S1[x, y, i] = s1
             f0[x + 2, y, i] = fl0
             f1[x, y + 2, i] = fl1
@@ -505,7 +523,7 @@
         return carry
 
     lax.fori_loop(0, bx, assemble, 0)
-    for c in copies + near_y[0] + near_y[1] + first + second:
+    for c in copies + near_y[0] + near_y[1] + near_x + first + second:
         c.wait_send()
     mine = acc2[gy]
     for d, c in enumerate(second):
@@ -555,7 +573,7 @@
             v32(4, bx + 4, by + 4, nocc, lanes),
             v32(4, bx + 4, by + 4, nvir, lanes),
         ]
-        + [v32(bx, by, nocc, nvir, lanes)] * 6
+        + [v32(bx, by, nocc, nvir, lanes)] * 5
         + [
             v32(4, 4, nocc, nvir, lanes),
             v32(bx + 4, by, nocc, nvir, lanes),
@@ -569,7 +587,7 @@
             v32(nx, ny, nz, rows, pairs),
             v32(nx * nz, ny, rows, pairs),
             v32(ny, rows, pairs), v32(ny, rows, pairs),
-            dma(28), dma(28), dma(4), dma(4), dma(4), dma(nx * nz), dma(nx * nz), dma(ny), dma(ny),
+            dma(28), dma(28), dma(6), dma(6), dma(4), dma(nx * nz), dma(nx * nz), dma(ny), dma(ny),
         ],
         compiler_params=pltpu.CompilerParams(
             collective_id=0, has_side_effects=True, vmem_limit_bytes=54 * MIB

time: 28.5 us -> 28.2 us (0.989)
  Pallas kernels: 27.7 us -> 27.4 us
where the time goes in v7:
time: 28.2 us; the launch traced here: 28.1 us
  Pallas kernels  27.4 us (97%)
  between operations  0.64 us (2%)
    pallas_call x1, Pallas kernels, on_device(): pl.pallas_call(flow_kernel, out_shape=(v32(pairs * cells, lanes), v32(row...  26.1 us
    pallas_call x1, Pallas kernels, on_device(): pl.pallas_call(write_kernel, out_shape=(sds(pairs * cells, lanes), sds(ro...  1.39 us

profile of v7, /device:TPU:0, one launch (start us, length us, event | category | flops | bytes accessed | tf_op | source)
XLA Modules:
  0.0 28.1 jit_solution(6872200274416589244)
XLA Ops:
  0.6 26.1 %flow.1 = (f32[4096,128]{1,0:T(8,128)S(1)}, f32[8,256]{1,0:T(8,128)S(1)}) custom-call(f32[256,128]{1,0:T(8,128)} %bitcast.5, f32[256,128]{1,0:T(8,128)} %bitcast.6, f32[64,128]{1,0:T(8,128)} %bitcast.7, f32[48,128]{1,0:T(8,128)} %bitcast.8), custom_call_target="tpu_custom_call" | custom-call | tf_op jit(solution)/shard_map/flow/pallas_call | solution.py:564
  26.7 1.4 %write.1 = (f32[4096,128]{1,0:T(8,128)}, f32[8,256]{1,0:T(8,128)}) custom-call(f32[4096,128]{1,0:T(8,128)S(1)} %get-tuple-element.6.pot_in, f32[8,256]{1,0:T(8,128)S(1)} %get-tuple-element.7.cas_in), custom_call_target="tpu_custom_call" | custom-call | tf_op jit(solution)/shard_map/write/pallas_call | solution.py:597

commit v8 on v7

--- a/solution.py
+++ b/solution.py
@@ -210,6 +210,13 @@
 
     multiply(cells, lambda t: (4 + t // by, 4 + lax.rem(t, by)))
 
+    def low_pass(x, carry):
+        for y in range(by):
+            for i in range(nocc):
+                NL[x, y, i] = rest(N[x + 4, y + 2, i])
+        return carry
+
+    lax.fori_loop(0, bx, low_pass, 0)
     for c in z_in:
         c.wait_recv()
     low = (lanes_of((nocc, lanes)) & 3) < 2
@@ -260,7 +267,6 @@
         for y in range(by):
             shifted = [vS[k, x + 2, y + 2] for k in range(4)]
             for i in range(nocc):
-                NL[x, y, i] = rest(n_at(x, y, i))
                 S2[x, y, i] = slope_z(x, y, i, shifted)
         return carry
 
@@ -464,7 +470,7 @@
                 f1[x, b, i] = (c0 * s0 + c1 * s1) + (slope_z(x, y, i, shifted) + c3 * n(0))
         return carry
 
-    lax.fori_loop(0, bx, at_y, 0)
+    lax.fori_loop(0, bx - 1, at_y, 0)
 
     for c in first:
         c.wait_recv()
@@ -483,6 +489,7 @@
         c.start()
         second.append(c)
 
+    lax.fori_loop(bx - 1, bx, at_y, 0)
     for c in z_out:
         c.wait_recv()
     for j in range(nocc // 2):

time: 28.2 us -> 27.9 us (0.989)
  Pallas kernels: 27.4 us -> 27.1 us
    pallas_call x1, Pallas kernels: 26.1 us -> 25.7 us  [on_device(): pl.pallas_call(flow_kernel, out_shape=(v32(pairs * cells, lanes), v32(row...]
where the time goes in v8:
time: 27.9 us; the launch traced here: 27.7 us
  Pallas kernels  27.1 us (97%)
  between operations  0.64 us (2%)
    pallas_call x1, Pallas kernels, on_device(): pl.pallas_call(flow_kernel, out_shape=(v32(pairs * cells, lanes), v32(row...  25.7 us
    pallas_call x1, Pallas kernels, on_device(): pl.pallas_call(write_kernel, out_shape=(sds(pairs * cells, lanes), sds(ro...  1.39 us

profile of v8, /device:TPU:0, one launch (start us, length us, event | category | flops | bytes accessed | tf_op | source)
XLA Modules:
  0.0 27.7 jit_solution(16259536539252509822)
XLA Ops:
  0.6 25.7 %flow.1 = (f32[4096,128]{1,0:T(8,128)S(1)}, f32[8,256]{1,0:T(8,128)S(1)}) custom-call(f32[256,128]{1,0:T(8,128)} %bitcast.5, f32[256,128]{1,0:T(8,128)} %bitcast.6, f32[64,128]{1,0:T(8,128)} %bitcast.7, f32[48,128]{1,0:T(8,128)} %bitcast.8), custom_call_target="tpu_custom_call" | custom-call | tf_op jit(solution)/shard_map/flow/pallas_call | solution.py:571
  26.4 1.4 %write.1 = (f32[4096,128]{1,0:T(8,128)}, f32[8,256]{1,0:T(8,128)}) custom-call(f32[4096,128]{1,0:T(8,128)S(1)} %get-tuple-element.6.pot_in, f32[8,256]{1,0:T(8,128)S(1)} %get-tuple-element.7.cas_in), custom_call_target="tpu_custom_call" | custom-call | tf_op jit(solution)/shard_map/write/pallas_call | solution.py:604
